TPU v7x, 8 devices: a whole 2x2x1 slice. The times are simulated.
8 devices in a mesh: dp: 1 (over z), fsdp: 2 (over y), sp: 4 (over x, core).
Axes of the slice: x: 2, y: 2, z: 1, core: 2. Of those that a mesh axis runs over, the one named last changes fastest.
Arguments:
- x_in: bfloat16 [32, 512, 4096], P(('dp', 'fsdp'), 'sp')
- norm_attn: bfloat16 [4096], P('fsdp')
- w_query: bfloat16 [4096, 4096], P('fsdp')
- w_key: bfloat16 [4096, 4096], P('fsdp')
- w_value: bfloat16 [4096, 4096], P('fsdp')
- w_out: bfloat16 [4096, 4096], P('fsdp')
- norm_mlp: bfloat16 [4096], P('fsdp')
- w_gate: bfloat16 [4096, 11008], P('fsdp')
- w_up: bfloat16 [4096, 11008], P('fsdp')
- w_down: bfloat16 [11008, 4096], P('fsdp')
Outputs:
- output: bfloat16 [32, 512, 4096], P(('dp', 'fsdp'), 'sp')
All inputs are finite; a program needn't handle non-finite values.
Results may differ from a plain program's by a relative error of at most 0.0114426.
Values are sent between devices in bfloat16 or wider.
A program may use at most 1 GiB of HBM per device.

v0:
```python
import math
import functools
import jax
import jax.numpy as jnp
from jax import lax
from jax.sharding import PartitionSpec as P

HEAD_DIM = 128
NORM_EPS = 1e-5
ROPE_THETA = 5e7
MASK_VALUE = -1e30


def rms_norm(hidden, gain):
    hid_f32 = hidden.astype(jnp.float32)
    inv_rms = lax.rsqrt(jnp.mean(hid_f32 * hid_f32, axis=-1, keepdims=True) + NORM_EPS)
    return (hid_f32 * inv_rms * gain.astype(jnp.float32)).astype(jnp.bfloat16)


def apply_rope(proj, angles):
    half_dim = proj.shape[-1] // 2
    lower_half = proj[..., :half_dim]
    upper_half = proj[..., half_dim:]
    cos_tab = jnp.cos(angles)[..., None, :]
    sin_tab = jnp.sin(angles)[..., None, :]
    return jnp.concatenate([lower_half * cos_tab - upper_half * sin_tab, upper_half * cos_tab + lower_half * sin_tab], axis=-1)


def rope_angles(token_pos):
    inv_freq = jnp.exp(jnp.arange(HEAD_DIM // 2, dtype=jnp.float32) * (-2.0 * math.log(ROPE_THETA) / HEAD_DIM))
    return token_pos.astype(jnp.float32)[:, None] * inv_freq[None, :]


def gather_weight(weight_shard):
    return lax.all_gather(weight_shard, 'fsdp', axis=0, tiled=True)


def local_layer(x_loc, norm_attn, w_query, w_key, w_value, w_out, norm_mlp, w_gate, w_up, w_down, num_shards):
    num_rows, shard_len, model_dim = x_loc.shape
    head_shape = (num_rows, shard_len, model_dim // HEAD_DIM, HEAD_DIM)
    pos_loc = jnp.arange(shard_len, dtype=jnp.int32) * num_shards + lax.axis_index('sp')
    seq_idx = jnp.arange(num_shards * shard_len, dtype=jnp.int32)
    pos_all = (seq_idx % shard_len) * num_shards + seq_idx // shard_len
    angles = rope_angles(pos_loc)
    normed = rms_norm(x_loc, gather_weight(norm_attn))
    query_rot = apply_rope(jnp.dot(normed, gather_weight(w_query), preferred_element_type=jnp.float32).reshape(head_shape), angles).astype(jnp.bfloat16)
    key_rot = apply_rope(jnp.dot(normed, gather_weight(w_key), preferred_element_type=jnp.float32).reshape(head_shape), angles).astype(jnp.bfloat16)
    value_loc = jnp.dot(normed, gather_weight(w_value), preferred_element_type=jnp.float32).astype(jnp.bfloat16).reshape(head_shape)
    key_all = lax.all_gather(key_rot, 'sp', axis=1, tiled=True)
    value_all = lax.all_gather(value_loc, 'sp', axis=1, tiled=True)
    scores = jnp.einsum('bqhd,bkhd->bhqk', query_rot, key_all, preferred_element_type=jnp.float32) * HEAD_DIM ** -0.5
    allowed = pos_all[None, None, None, :] <= pos_loc[None, None, :, None]
    attn_prob = jax.nn.softmax(jnp.where(allowed, scores, MASK_VALUE), axis=-1).astype(jnp.bfloat16)
    attn_mix = jnp.einsum('bhqk,bkhd->bqhd', attn_prob, value_all, preferred_element_type=jnp.float32).astype(jnp.bfloat16).reshape(num_rows, shard_len, model_dim)
    resid = (x_loc.astype(jnp.float32) + jnp.dot(attn_mix, gather_weight(w_out), preferred_element_type=jnp.float32)).astype(jnp.bfloat16)
    normed_mlp = rms_norm(resid, gather_weight(norm_mlp))
    gate_act = jax.nn.silu(jnp.dot(normed_mlp, gather_weight(w_gate), preferred_element_type=jnp.float32))
    up_proj = jnp.dot(normed_mlp, gather_weight(w_up), preferred_element_type=jnp.float32)
    hidden_mlp = (gate_act * up_proj).astype(jnp.bfloat16)
    return (resid.astype(jnp.float32) + jnp.dot(hidden_mlp, gather_weight(w_down), preferred_element_type=jnp.float32)).astype(jnp.bfloat16)


def solution(mesh):
    row_spec = P(('dp', 'fsdp'), 'sp', None)
    weight_spec = P('fsdp', None)
    gain_spec = P('fsdp')
    in_specs = (row_spec, gain_spec, weight_spec, weight_spec, weight_spec, weight_spec, gain_spec, weight_spec, weight_spec, weight_spec)
    layer_fn = functools.partial(local_layer, num_shards=mesh.shape['sp'])
    return jax.shard_map(layer_fn, mesh=mesh, in_specs=in_specs, out_specs=row_spec, check_vma=False)
```

profile of v0, /device:TPU:0, one launch (start us, length us, event | category | flops | bytes accessed | tf_op | source)
XLA Modules:
  0.0 5654.4 jit_solution(10075332166040550913)
XLA Ops:
  6.5 0.7 all-gather.14.cloned.1.call-update
  7.3 0.7 all-gather.16.cloned.1.call-update
  8.8 5.7 all_gather.33
  14.5 7.2 fusion.13
  21.7 0.9 multiply_cosine_fusion
  22.7 374.5 %all-gather.14.cloned.1.call-done = bf16[4096,4096]{1,0:T(8,128)(2,1)} async-done(((bf16[2048,4096]{1,0:T(8,128)(2,1)}), bf16[4096,4096]{1,0:T(8,128)(2,1)}) %all-gather.14.cloned.1.call-update) | async-done | bytes 33554448 | tf_op jit(solution)/shard_map/all_gather | solution.py:35
  397.2 78.7 %fusion.25 = f32[16,128,4096]{2,1,0:T(8,128)} fusion(bf16[4096,4096]{1,0:T(8,128)(2,1)} %all-gather.14.cloned.1.call-done, bf16[16,128,4096]{2,1,0:T(8,128)(2,1)} %param.10, f32[4096]{0:T(1024)S(1)} %convert_element_type.51, f32[16,128]{1,0:T(8,128)S(1)} %add_rsqrt_fusion.1), kind=kOutput, calls=%fused_computation.35 | convolution fusion | flops 68753031168 | bytes 83910656 | tf_op jit(solution)/shard_map/dot_general | solution.py:46
  475.9 27.6 copy.29
  503.5 280.8 %all-gather.16.cloned.1.call-done = bf16[4096,4096]{1,0:T(8,128)(2,1)} async-done(((bf16[2048,4096]{1,0:T(8,128)(2,1)}), bf16[4096,4096]{1,0:T(8,128)(2,1)}) %all-gather.16.cloned.1.call-update) | async-done | bytes 33554448 | tf_op jit(solution)/shard_map/all_gather | solution.py:35
  784.3 79.1 %fusion.23 = f32[16,128,4096]{2,1,0:T(8,128)} fusion(bf16[4096,4096]{1,0:T(8,128)(2,1)} %all-gather.16.cloned.1.call-done, bf16[16,128,4096]{2,1,0:T(8,128)(2,1)} %param.10, f32[4096]{0:T(1024)S(1)} %convert_element_type.51, f32[16,128]{1,0:T(8,128)S(1)} %add_rsqrt_fusion.1), kind=kOutput, calls=%fused_computation.33 | convolution fusion | flops 68753031168 | bytes 83910656 | tf_op jit(solution)/shard_map/dot_general | solution.py:47
  863.4 27.6 copy.30
  890.9 84.2 %fusion.60 = (f32[16,128,32,64]{3,2,1,0:T(8,128)}, f32[16,128,32,64]{3,2,1,0:T(8,128)}, f32[16,128,32,64]{3,2,1,0:T(8,128)}, f32[16,128,32,64]{3,2,1,0:T(8,128)}) fusion(f32[16,128,32,128]{3,2,1,0:T(8,128)} %bitcast.50, f32[16,128,32,128]{3,2,1,0:T(8,128)} %bitcast.51), kind=kLoop, calls=%fused_computation.75 | loop fusion | bytes 134217728 | tf_op jit(solution)/shard_map/slice | solution.py:22
  975.1 163.8 %subtract_convert_fusion.1 = (bf16[16,128,32,64]{3,1,2,0:T(8,128)(2,1)}, bf16[16,128,32,64]{3,1,2,0:T(8,128)(2,1)}, bf16[16,128,32,64]{3,1,2,0:T(8,128)(2,1)}, bf16[16,128,32,64]{3,1,2,0:T(8,128)(2,1)}) fusion(f32[16,128,32,64]{3,2,1,0:T(8,128)} %get-tuple-element.10, f32[16,128,32,64]{3,2,1,0:T(8,128)} %get-tuple-element.9, f32[128,64]{1,0:T(8,128)S(1)} %copy-done.1, ...), kind=kLoop, calls=%fused_computation.42 | loop fusion | flops 67108864 | bytes 100728832 | tf_op jit(solution)/shard_map/convert.2
  1138.9 20.8 pad_maximum_fusion
  1159.8 11.5 all-gather.10.cloned.1.call-done
  1171.4 82.6 %fusion.37 = bf16[16,128,4096]{2,1,0:T(8,128)(2,1)} fusion(bf16[4096,4096]{1,0:T(8,128)(2,1)} %all-gather.10.cloned.1.call-done, bf16[16,128,4096]{2,1,0:T(8,128)(2,1)} %param.10, f32[4096]{0:T(1024)S(1)} %copy-done.3, f32[16,128]{1,0:T(8,128)S(1)} %copy-done.6), kind=kOutput, calls=%fused_computation.48 | convolution fusion | flops 68761419776 | bytes 67133440 | tf_op jit(solution)/shard_map/dot_general | solution.py:48
  1254.0 21.2 copy.24
  1276.6 0.7 all-gather.24.cloned.1.call-update
  1278.1 4.3 all_gather.40
  1283.1 279.3 %all-gather.18.cloned.1.call-done = bf16[16,512,32,128]{3,1,2,0:T(8,128)(2,1)} async-done(((bf16[16,128,32,128]{3,1,2,0:T(8,128)(2,1)}), bf16[16,512,32,128]{3,1,2,0:T(8,128)(2,1)}) %all-gather.18.cloned.1.call-update) | async-done | bytes 67108880 | tf_op jit(solution)/shard_map/all_gather | solution.py:49
  1562.4 81.1 %fusion.29 = f32[16,32,128,512]{3,2,1,0:T(8,128)} fusion(bf16[16,512,32,128]{3,1,2,0:T(8,128)(2,1)} %all-gather.18.cloned.1.call-done, bf16[16,128,32,64]{3,1,2,0:T(8,128)(2,1)} %get-tuple-element.6, bf16[16,128,32,64]{3,1,2,0:T(8,128)(2,1)} %get-tuple-element.5), kind=kOutput, calls=%fused_computation.43 | convolution fusion | flops 8623489024 | bytes 218103808 | tf_op jit(solution)/shard_map/bqhd,bkhd->bhqk/dot_general | solution.py:51
  1643.6 132.0 %fusion.62 = (f32[16,32,128]{2,1,0:T(8,128)S(1)}, f32[16,32,128,512]{3,2,1,0:T(8,128)}) fusion(f32[16,32,128,512]{3,2,1,0:T(8,128)} %fusion.29, pred[128,512]{1,0:T(8,128)(4,1)S(1)} %broadcast_compare_fusion), kind=kOutput, calls=%fused_computation.77 | output fusion | flops 201327104 | bytes 268763136 | tf_op jit(solution)/shard_map/sub | solution.py:53
  1775.5 187.0 %all-gather.12.cloned.1.call-done = bf16[16,512,32,128]{1,3,2,0:T(8,128)(2,1)} async-done(((bf16[16,128,32,128]{1,3,2,0:T(8,128)(2,1)}), bf16[16,512,32,128]{1,3,2,0:T(8,128)(2,1)}) %all-gather.12.cloned.1.call-update) | async-done | bytes 67108880 | tf_op jit(solution)/shard_map/all_gather | solution.py:50
  1962.5 67.1 %fusion.42 = bf16[16,32,128,128]{3,2,1,0:T(8,128)(2,1)} fusion(bf16[16,512,32,128]{1,3,2,0:T(8,128)(2,1)} %all-gather.12.cloned.1.call-done, f32[16,32,128,512]{3,2,1,0:T(8,128)} %get-tuple-element.18, f32[16,32,128]{2,1,0:T(8,128)S(1)} %get-tuple-element.17), kind=kOutput, calls=%fused_computation.49 | convolution fusion | flops 8665432064 | bytes 218365952 | tf_op jit(solution)/shard_map/bhqk,bkhd->bqhd/dot_general | solution.py:54
  2029.6 319.9 %all-gather.20.cloned.1.call-done = bf16[4096,4096]{1,0:T(8,128)(2,1)} async-done(((bf16[2048,4096]{1,0:T(8,128)(2,1)}), bf16[4096,4096]{1,0:T(8,128)(2,1)}) %all-gather.20.cloned.1.call-update) | async-done | bytes 33554448 | tf_op jit(solution)/shard_map/all_gather | solution.py:35
  2349.4 83.3 %fusion.17 = (f32[16,128]{1,0:T(8,128)S(1)}, bf16[16,128,4096]{2,1,0:T(8,128)(2,1)}) fusion(bf16[16,128,4096]{1,2,0:T(8,128)(2,1)} %bitcast.55, bf16[4096,4096]{1,0:T(8,128)(2,1)} %all-gather.20.cloned.1.call-done, bf16[16,128,4096]{2,1,0:T(8,128)(2,1)} %param.10), kind=kOutput, calls=%fused_computation.27 | convolution fusion | flops 68769808384 | bytes 83894272 | tf_op jit(solution)/shard_map/dot_general | solution.py:55
  2432.7 941.6 %all-gather.22.cloned.1.call-done = bf16[4096,11008]{1,0:T(8,128)(2,1)} async-done(((bf16[2048,11008]{1,0:T(8,128)(2,1)}), bf16[4096,11008]{1,0:T(8,128)(2,1)}) %all-gather.22.cloned.1.call-update) | async-done | bytes 90177552 | tf_op jit(solution)/shard_map/all_gather | solution.py:35
  3374.3 205.9 %fusion.6 = f32[16,128,11008]{2,1,0:T(8,128)} fusion(bf16[4096,11008]{1,0:T(8,128)(2,1)} %all-gather.22.cloned.1.call-done, bf16[16,128,4096]{2,1,0:T(8,128)(2,1)} %get-tuple-element.20, f32[4096]{0:T(1024)S(1)} %copy-done.4, f32[16,128]{1,0:T(8,128)S(1)} %add_rsqrt_fusion), kind=kOutput, calls=%fused_computation.9 | convolution fusion | flops 184717148160 | bytes 197156864 | tf_op jit(solution)/shard_map/dot_general | solution.py:57
  3580.1 819.0 %all-gather.24.cloned.1.call-done = bf16[4096,11008]{1,0:T(8,128)(2,1)} async-done(((bf16[2048,11008]{1,0:T(8,128)(2,1)}), bf16[4096,11008]{1,0:T(8,128)(2,1)}) %all-gather.24.cloned.1.call-update) | async-done | bytes 90177552 | tf_op jit(solution)/shard_map/all_gather | solution.py:35
  4399.1 206.1 %fusion.4 = f32[16,128,11008]{2,1,0:T(8,128)} fusion(bf16[4096,11008]{1,0:T(8,128)(2,1)} %all-gather.24.cloned.1.call-done, bf16[16,128,4096]{2,1,0:T(8,128)(2,1)} %get-tuple-element.20, f32[4096]{0:T(1024)S(1)} %copy-done.4, f32[16,128]{1,0:T(8,128)S(1)} %add_rsqrt_fusion), kind=kOutput, calls=%fused_computation.7 | convolution fusion | flops 184717148160 | bytes 197156864 | tf_op jit(solution)/shard_map/dot_general | solution.py:58
  4605.2 818.8 %all-gather.26.cloned.1.call-done = bf16[11008,4096]{1,0:T(8,128)(2,1)} async-done(((bf16[5504,4096]{1,0:T(8,128)(2,1)}), bf16[11008,4096]{1,0:T(8,128)(2,1)}) %all-gather.26.cloned.1.call-update) | async-done | bytes 90177552 | tf_op jit(solution)/shard_map/all_gather | solution.py:35
  5424.0 223.8 %fusion.20 = bf16[16,128,4096]{2,1,0:T(8,128)(2,1)} fusion(bf16[16,128,4096]{2,1,0:T(8,128)(2,1)} %get-tuple-element.20, bf16[11008,4096]{1,0:T(8,128)(2,1)} %all-gather.26.cloned.1.call-done, f32[16,128,11008]{2,1,0:T(8,128)} %fusion.4, f32[16,128,11008]{2,1,0:T(8,128)} %fusion.6), kind=kOutput, calls=%fused_computation.30 | convolution fusion | flops 184844025856 | bytes 304087040 | tf_op jit(solution)/shard_map/dot_general | solution.py:60
  (42 shorter events, 3.7 us)
Async XLA Ops:
  6.5 2.3 copy-start.7
  6.5 390.7 %all-gather.14.cloned.1.call-start = ((), (), s32[]{:S(2)}) async-start(), calls=%async_computation.2 | async-start | bytes 50331648 | tf_op jit(solution)/shard_map/all_gather | solution.py:35
  7.3 777.0 %all-gather.16.cloned.1.call-start = ((), (), s32[]{:S(2)}) async-start(), calls=%async_computation.3 | async-start | bytes 50331648 | tf_op jit(solution)/shard_map/all_gather | solution.py:35
  8.0 1163.3 %all-gather.10.cloned.1.call-start = ((), (), s32[]{:S(2)}) async-start(), calls=%async_computation | async-start | bytes 50331648 | tf_op jit(solution)/shard_map/all_gather | solution.py:35
  8.7 1553.7 %all-gather.18.cloned.1.call-start = ((), (), s32[]{:S(2)}) async-start(), calls=%async_computation.4 | async-start | bytes 83886080 | tf_op jit(solution)/shard_map/all_gather | solution.py:49
  14.5 769.8 %copy-start.2 = (f32[4096]{0:T(1024)}, f32[4096]{0:T(1024)S(1)}, u32[]{:S(2)}) copy-start(f32[4096]{0:T(1024)S(1)} %convert_element_type.51) | copy-start | bytes 49156
  21.7 762.6 %copy-start.5 = (f32[16,128]{1,0:T(8,128)}, f32[16,128]{1,0:T(8,128)S(1)}, u32[]{:S(2)}) copy-start(f32[16,128]{1,0:T(8,128)S(1)} %add_rsqrt_fusion.1) | copy-start | bytes 24580
  890.9 84.2 %copy-start = (f32[128,64]{1,0:T(8,128)S(1)}, f32[128,64]{1,0:T(8,128)}, u32[]{:S(2)}) copy-start(f32[128,64]{1,0:T(8,128)} %get-tuple-element.15) | copy-start | bytes 98308
  890.9 84.2 %copy-start.1 = (f32[128,64]{1,0:T(8,128)S(1)}, f32[128,64]{1,0:T(8,128)}, u32[]{:S(2)}) copy-start(f32[128,64]{1,0:T(8,128)} %get-tuple-element.16) | copy-start | bytes 98308
  1138.9 32.4 copy-start.3
  1138.9 32.4 copy-start.6
  1159.8 802.7 %all-gather.12.cloned.1.call-start = ((), (), s32[]{:S(2)}) async-start(), calls=%async_computation.1 | async-start | bytes 83886080 | tf_op jit(solution)/shard_map/all_gather | solution.py:50
  1275.2 1074.2 %all-gather.20.cloned.1.call-start = ((), (), s32[]{:S(2)}) async-start(), calls=%async_computation.5 | async-start | bytes 50331648 | tf_op jit(solution)/shard_map/all_gather | solution.py:35
  1275.8 2098.5 %all-gather.22.cloned.1.call-start = ((), (), s32[]{:S(2)}) async-start(), calls=%async_computation.6 | async-start | bytes 135266304 | tf_op jit(solution)/shard_map/all_gather | solution.py:35
  1276.5 3122.6 %all-gather.24.cloned.1.call-start = ((), (), s32[]{:S(2)}) async-start(), calls=%async_computation.7 | async-start | bytes 135266304 | tf_op jit(solution)/shard_map/all_gather | solution.py:35
  1277.3 0.8 copy-start.8
  1277.3 4146.7 %all-gather.26.cloned.1.call-start = ((), (), s32[]{:S(2)}) async-start(), calls=%async_computation.8 | async-start | bytes 135266304 | tf_op jit(solution)/shard_map/all_gather | solution.py:35
  2349.4 1024.8 %copy-start.4 = (f32[4096]{0:T(1024)S(1)}, f32[4096]{0:T(1024)}, u32[]{:S(2)}) copy-start(f32[4096]{0:T(1024)} %convert_element_type.60) | copy-start | bytes 49156
Sparse Core Ops, SparseCore 0:
  8.8 388.3 all-gather.13
  398.7 385.4 all-gather.15
  785.8 385.4 all-gather.9
  1172.7 389.6 all-gather.17
  1563.8 398.6 all-gather.11
  1963.9 385.4 all-gather.19
  2351.0 1023.2 all-gather.21
  3375.8 1023.2 all-gather.23
  4400.6 1023.2 all-gather.25
where the time goes:
time: 5660 us; the launch traced here: 5650 us
  waiting for transfers between devices  4040 us (71%)
  matrix products  1110 us (20%)
  other arithmetic  325 us (6%)
  local copies, waits for them, and re-layouts  161 us (3%)
    all_gather x7, waiting for transfers between devices, gather_weight(): return lax.all_gather(weight_shard, 'fsdp', axis=0, tiled=True)  3570 us
    all_gather x1, waiting for transfers between devices, local_layer(): key_all = lax.all_gather(key_rot, 'sp', axis=1, tiled=True)  279 us
    dot_general x1, matrix products, local_layer(): jnp.dot(hidden_mlp, gather_weight(w_down), preferred_element_type=jnp.flo...  224 us
    dot_general x1, matrix products, local_layer(): jnp.dot(normed_mlp, gather_weight(w_up), preferred_element_type=jnp.float32)  206 us
    dot_general x1, matrix products, local_layer(): jnp.dot(normed_mlp, gather_weight(w_gate), preferred_element_type=jnp.flo...  206 us
    all_gather x1, waiting for transfers between devices, local_layer(): value_all = lax.all_gather(value_loc, 'sp', axis=1, tiled=True)  187 us
    another operation x1, other arithmetic  164 us
    sub x1, other arithmetic, local_layer(): jax.nn.softmax(jnp.where(allowed, scores, MASK_VALUE), axis=-1)  132 us
  transfers between devices with their start and end apart: 9, of which 9 were waited for; matrix products, arithmetic and copies ran while one was open for 24% of the time, Pallas kernels for 0%

commit v1 on v0

v1 whole, which is shorter than its diff:
```python
import math
import functools
import jax
import jax.numpy as jnp
from jax import lax
from jax.experimental import pallas as pl
from jax.experimental.pallas import tpu as pltpu
from jax.sharding import PartitionSpec as P

HEAD = 128
EPS = 1e-5
THETA = 5e7
NEG = -1e30
BF = jnp.bfloat16
F32 = jnp.float32
MESH = pl.DeviceIdType.MESH

D = 4096
HD = D // 2
FFN = 11008
HF = FFN // 2
TOK = 2048
CW = 512
FW = 256

NC, NE, NF, NG = 24, 8, 43, 16
E0 = NC
F0 = E0 + NE
G0 = F0 + NF
N = G0 + NG
NSEM = NC + NE + 2 * NF + NG
DIRECT = 7
C_E, C_M = 256, 512
YAHEAD = 12
SLOTS = 6
KB = 1024
KSPLIT = ((0, 2816), (2816, 5632), (5632, 8448), (8448, FFN))


def kernel(x_in, gown, cos, sin, qpos, kpos, wq, wk, wv, wo, wg, wu, wd,
           y, xr, rq, rk, rv, ro, rg, ru, rd, ob, ubuf, hbuf,
           grem, ys, yr, xs, xrs, dys, dyr, dxs, dxr, gsem, xsend, xrecv, osend, orecv):
    f = lax.axis_index('fsdp')
    s = lax.axis_index('sp')
    cx = s // 2
    cc = s % 2
    ynbr = (0, 1 - f, s)
    xnbr = (0, f, (s + 2) % 4)
    pnbr = (0, f, cx * 2 + 1 - cc)

    def peer(k):
        if k == 1:
            return cx * 2 + 1 - cc
        if k == 2:
            return (s + 2) % 4
        return 3 - s

    bar = pltpu.get_barrier_semaphore()
    for dev in (ynbr, pnbr, xnbr, (0, f, 3 - s)):
        pl.semaphore_signal(bar, inc=1, device_id=dev, device_id_type=MESH)
    pl.semaphore_wait(bar, 4)

    def rcopy(src, dst, ssem, rsem, dev):
        return pltpu.make_async_remote_copy(src_ref=src, dst_ref=dst, send_sem=ssem, recv_sem=rsem, device_id=dev, device_id_type=MESH)

    class Part:
        def __init__(self, w, r, col, ncol, half, e, m, sem):
            self.w, self.r, self.half, self.e, self.m, self.sem = w, r, half, e, m, sem
            self.cols = pl.ds(col, ncol)

        def rows(self, off, n):
            return pl.ds(pl.multiple_of(cc * self.half + off, 32), n)

        def ycopy(self):
            a = (self.rows(cx * self.e, self.e + self.m), self.cols)
            return rcopy(self.w.at[a], self.r.at[a], ys.at[self.sem], yr.at[self.sem], ynbr)

        def xcopy(self):
            a = (self.rows(cx * (self.e + self.m), self.e), self.cols)
            return rcopy(self.r.at[a], self.r.at[a], xs.at[self.sem], xrs.at[self.sem], xnbr)

        def dycopy(self):
            a = (self.rows(cx * self.e, self.e + self.m), self.cols)
            return rcopy(self.r.at[a], self.r.at[a], dys.at[self.sem], dyr.at[self.sem], pnbr)

        def dxcopy(self):
            a = (self.rows((1 - cx) * (self.e + self.m), self.e), self.cols)
            return rcopy(self.r.at[a], self.r.at[a], dxs.at[self.sem], dxr.at[self.sem], pnbr)

        def ysend(self):
            self.ycopy().start()

        def yf(self):
            c = self.ycopy()
            c.wait_recv()
            if self.e:
                self.xcopy().start()
            self.dycopy().start()
            c.wait_send()

        def xf(self):
            if self.e:
                c = self.xcopy()
                c.wait_recv()
                self.dxcopy().start()
                c.wait_send()

        def done(self):
            c = self.dycopy()
            c.wait_recv()
            c.wait_send()
            if self.e:
                c = self.dxcopy()
                c.wait_recv()
                c.wait_send()

    def al(v, k):
        return v if isinstance(v, int) else pl.multiple_of(v, k)

    def when(cond, fn):
        if isinstance(cond, bool):
            if cond:
                fn()
        else:
            pl.when(cond)(fn)

    def item(n, what, cand):
        if 'C' in cand:
            for j, (w, r) in enumerate(((wq, rq), (wk, rk), (wv, rv))):
                col = al((n // 3) * CW, CW)
                if 'D' in cand:
                    when((n < DIRECT) & (n % 3 == j), lambda: getattr(Part(w, r, col, CW, HD // 2, 0, HD // 2, n), what)())
                when((n >= DIRECT) & (n < E0) & (n % 3 == j), lambda: getattr(Part(w, r, col, CW, HD // 2, C_E, C_M, n), what)())
        if 'E' in cand:
            when((n >= E0) & (n < F0), lambda: getattr(Part(wo, ro, al((n - E0) * CW, CW), CW, HD // 2, HD // 4, 0, n), what)())
        if 'F' in cand:
            def both():
                col = al((n - F0) * FW, FW)
                for i, (w, r) in enumerate(((wg, rg), (wu, ru))):
                    getattr(Part(w, r, col, FW, HD // 2, HD // 4, 0, F0 + 2 * (n - F0) + i), what)()
            when((n >= F0) & (n < G0), both)
        if 'G' in cand:
            when((n >= G0) & (n < N), lambda: getattr(Part(wd, rd, al((n - G0) * FW, FW), FW, HF // 2, HF // 4, 0, n + NF), what)())

    gcopy = rcopy(gown, grem, gsem.at[0], gsem.at[1], ynbr)
    gcopy.start()
    for n in range(3):
        item(n, 'ysend', 'CD')

    def xcopy(r, k):
        src = x_in.at[pl.ds(pl.multiple_of((peer(k) * 4 + r) * 128, 128), 128)]
        dst = xr.at[pl.ds(pl.multiple_of(r * 512 + s * 128, 128), 128)]
        return rcopy(src, dst, xsend.at[r, k - 1], xrecv.at[r, k - 1], (0, f, peer(k)))

    for r in range(4):
        for k in (2, 3, 1):
            xcopy(r, k).start()
    for n in range(3, YAHEAD):
        item(n, 'ysend', 'CD')
    gcopy.wait_recv()
    gcopy.wait_send()

    def scope(act, wbuf, obuf, wl, ol):
        def wcopies(n, cand):
            def go(fn):
                slot = n % SLOTS
                if 'C' in cand:
                    for j, (w, r) in enumerate(((wq, rq), (wk, rk), (wv, rv))):
                        a = (slice(None), pl.ds(al((n // 3) * CW, CW), CW))
                        when((n < E0) & (n % 3 == j), lambda: [fn(pltpu.make_async_copy(b.at[a], wbuf.at[slot, i], wl.at[slot, i])) for i, b in enumerate((w, r))] and None)
                if 'E' in cand:
                    a2 = (slice(None), pl.ds(al((n - E0) * CW, CW), CW))
                    when((n >= E0) & (n < F0), lambda: [fn(pltpu.make_async_copy(b.at[a2], wbuf.at[slot, i], wl.at[slot, i])) for i, b in enumerate((wo, ro))] and None)
                if 'F' in cand:
                    a3 = (slice(None), pl.ds(al((n - F0) * FW, FW), FW))

                    def ff():
                        for i, pair in enumerate(((wg, wu), (rg, ru))):
                            for j, b in enumerate(pair):
                                fn(pltpu.make_async_copy(b.at[a3], wbuf.at[slot, i, :, pl.ds(j * FW, FW)], wl.at[slot, i + 2 * j]))
                    when((n >= F0) & (n < G0), ff)
            return go

        def load(n, cand):
            wcopies(n, cand)(lambda c: c.start())

        def loaded(n, cand):
            wcopies(n, cand)(lambda c: c.wait())

        def project(rows, slot):
            acc = None
            for i in range(2):
                for k in range(0, HD, KB):
                    part = jnp.dot(act[i, rows, k:k + KB], wbuf[slot, i, k:k + KB], preferred_element_type=F32)
                    acc = part if acc is None else acc + part
            return acc

        def norm_tile(xt, t, row, g):
            def sub(i, _):
                rs = pl.ds(pl.multiple_of(i * 16, 16), 16)
                x0 = xt[t, 0, rs, :].astype(F32)
                x1 = xt[t, 1, rs, :].astype(F32)
                ss = jnp.sum(x0 * x0, axis=-1, keepdims=True) + jnp.sum(x1 * x1, axis=-1, keepdims=True)
                inv = lax.rsqrt(ss * (1.0 / D) + EPS)
                ro_ = pl.ds(pl.multiple_of(row + i * 16, 16), 16)
                act[0, ro_, :] = (xt[t, 0, rs, :].astype(F32) * inv * gown[pl.ds(g, 1), :]).astype(BF)
                act[1, ro_, :] = (xt[t, 1, rs, :].astype(F32) * inv * grem[pl.ds(g, 1), :]).astype(BF)
                return 0
            lax.fori_loop(0, 8, sub, 0)

        def halves(src, row, xt, t, sem):
            rows = pl.ds(row, 128)
            return [pltpu.make_async_copy(src.at[rows, pl.ds(pl.multiple_of(h * HD, HD), HD)], xt.at[t, i], sem.at[t, i])
                    for i, h in enumerate((f, 1 - f))]

        def attention_phase(xt, xl, qb, kb, vb):
            def tokens(r):
                for k in (1, 2, 3):
                    c = xcopy(r, k)
                    c.wait_recv()
                    c.wait_send()

                def cps(t):
                    return halves(xr, r * 512 + t * 128, xt, t, xl)
                for t in range(4):
                    @pl.when(s != t)
                    def _():
                        for c in cps(t):
                            c.start()

                    @pl.when(s == t)
                    def _():
                        for c in halves(x_in, pl.multiple_of((s * 4 + r) * 128, 128), xt, t, xl):
                            c.start()
                for t in range(4):
                    for c in cps(t):
                        c.wait()
                    norm_tile(xt, t, r * 512 + t * 128, 0)

            def ocopy(g, k):
                src = obuf.at[g % 2, pl.ds(pl.multiple_of(peer(k) * 512, 512), 512)]
                dst = ob.at[pl.ds(pl.multiple_of(s * 512, 512), 512), pl.ds(pl.multiple_of(g * CW, CW), CW)]
                return rcopy(src, dst, osend.at[g, k - 1], orecv.at[g, k - 1], (0, f, peer(k)))

            def olocal(g):
                return pltpu.make_async_copy(obuf.at[g % 2, pl.ds(pl.multiple_of(s * 512, 512), 512)],
                                             ob.at[pl.ds(pl.multiple_of(s * 512, 512), 512), pl.ds(pl.multiple_of(g * CW, CW), CW)], ol.at[g % 2])

            def rope(acc):
                out = []
                for h in range(CW // HEAD):
                    u = acc[:, h * HEAD:(h + 1) * HEAD]
                    out.append(u * cos[...] + pltpu.roll(u, HEAD // 2, 1) * sin[...])
                return jnp.concatenate(out, axis=1).astype(BF)

            def unit(q, _):
                g, r = q // 4, q % 4
                rows = pl.ds(pl.multiple_of(r * 512, 512), 512)

                @pl.when(r == 0)
                def _():
                    for j in range(3):
                        loaded(3 * g + j, 'C')

                    @pl.when(g >= 2)
                    def _():
                        for k in (1, 2, 3):
                            ocopy(g - 2, k).wait_send()
                        olocal(g - 2).wait()

                @pl.when(g == 0)
                def _():
                    tokens(r)

                base = (g % 2) * 3
                for j, (dst, fn) in enumerate(((qb, rope), (kb, rope), (vb, lambda a: a.astype(BF)))):
                    acc = project(rows, base + j)
                    dst[...] = fn(acc)

                def head(h, _):
                    hs = pl.ds(pl.multiple_of(h * HEAD, HEAD), HEAD)
                    sc = lax.dot_general(qb[:, hs], kb[:, hs], (((1,), (1,)), ((), ())), preferred_element_type=F32)
                    qp = qpos[...]
                    sc = jnp.where(jnp.concatenate([qp] * 4, axis=1) >= kpos[...], sc, NEG)
                    mx = jnp.max(sc, axis=-1, keepdims=True)
                    p = jnp.exp2((sc - mx) * (HEAD ** -0.5 * math.log2(math.e)))
                    tot = jnp.sum(p, axis=-1, keepdims=True)
                    o = jnp.dot(p.astype(BF), vb[:, hs], preferred_element_type=F32) / tot
                    o = o.astype(BF)
                    for t in range(4):
                        obuf[g % 2, pl.ds(pl.multiple_of(t * 512 + r * 128, 128), 128), hs] = o[t * 128:(t + 1) * 128]
                    return 0
                lax.fori_loop(0, CW // HEAD, head, 0)

                for qq, (yy, dd) in {0: ((3,), ()), 1: ((4,), (3,)), 2: ((5, 6, 7), (4,)), 3: ((8,), (5,))}.items():
                    @pl.when(q == qq)
                    def _():
                        for n in yy:
                            item(n, 'yf', 'CD')
                            item(n + YAHEAD - 3, 'ysend', 'CD')
                        for n in dd:
                            item(n, 'done', 'CD')
                            load(n, 'C')

                @pl.when((q >= 4) & (r < 3))
                def _():
                    n = 3 * g + 3 + r
                    item(n + YAHEAD, 'ysend', 'CEF')
                    item(n + 3, 'yf', 'CEF')
                    item(n + 1, 'xf', 'CE')
                    item(n, 'done', 'CDE')
                    load(n, 'CE')

                @pl.when(r == 3)
                def _():
                    for k in (2, 3, 1):
                        ocopy(g, k).start()
                    olocal(g).start()
                return 0

            for n in range(3):
                item(n, 'yf', 'CD')
                item(n, 'done', 'CD')
                load(n, 'C')
            lax.fori_loop(0, 32, unit, 0)
            for g in (6, 7):
                for k in (1, 2, 3):
                    ocopy(g, k).wait_send()
                olocal(g).wait()

            def arrived(g, _):
                for k in (1, 2, 3):
                    ocopy(g, k).wait_recv()
                return 0
            lax.fori_loop(0, 8, arrived, 0)

        pl.run_scoped(attention_phase, pltpu.VMEM((4, 2, 128, HD), BF), pltpu.SemaphoreType.DMA((4, 2)),
                      pltpu.VMEM((512, CW), BF), pltpu.VMEM((512, CW), BF), pltpu.VMEM((512, CW), BF))

        MT = 1024

        def out_phase(hx, hl, al_):
            def acopy(t, i):
                h = f if i == 0 else 1 - f
                rows = pl.ds(t * MT, MT)
                return pltpu.make_async_copy(ob.at[rows, pl.ds(pl.multiple_of(h * HD, HD), HD)], act.at[i, rows], al_.at[t, i])
            for t in range(TOK // MT):
                for i in range(2):
                    acopy(t, i).start()

            def xload(n):
                return pltpu.make_async_copy(x_in.at[:, pl.ds(pl.multiple_of((n - E0) * CW, CW), CW)], hx.at[n % 2], hl.at[n % 2])

            def hstore(n):
                return pltpu.make_async_copy(obuf.at[n % 2], hbuf.at[:, pl.ds(pl.multiple_of((n - E0) * CW, CW), CW)], ol.at[n % 2])

            xload(jnp.int32(E0)).start()
            for t in range(TOK // MT):
                for i in range(2):
                    acopy(t, i).wait()

            def step(n, _):
                item(n + YAHEAD + 3, 'ysend', 'EF')
                item(n + 6, 'yf', 'EF')
                item(n + 4, 'xf', 'EF')
                item(n + 3, 'done', 'EF')
                load(n + 3, 'EF')

                @pl.when(n + 1 < F0)
                def _():
                    xload(n + 1).start()

                @pl.when(n >= E0 + 2)
                def _():
                    hstore(n - 2).wait()
                loaded(n, 'E')
                xload(n).wait()
                slot = n % SLOTS

                def mt(t, _):
                    rows = pl.ds(pl.multiple_of(t * MT, MT), MT)
                    acc = project(rows, slot)
                    obuf[n % 2, rows, :] = (hx[n % 2, rows, :].astype(F32) + acc).astype(BF)
                    return 0
                lax.fori_loop(0, TOK // MT, mt, 0)
                hstore(n).start()
                return 0
            lax.fori_loop(E0, F0, step, 0)
            for n in (F0 - 2, F0 - 1):
                hstore(jnp.int32(n)).wait()

        pl.run_scoped(out_phase, pltpu.VMEM((2, TOK, CW), BF), pltpu.SemaphoreType.DMA((2,)), pltpu.SemaphoreType.DMA((2, 2)))

        def norm_phase(xt, xl):
            def cps(i):
                return halves(hbuf, pl.multiple_of(i * 128, 128), xt, i % 4, xl)
            for i in range(3):
                for c in cps(jnp.int32(i)):
                    c.start()

            def step(i, _):
                @pl.when(i + 3 < 16)
                def _():
                    for c in cps(i + 3):
                        c.start()
                for c in cps(i):
                    c.wait()
                norm_tile(xt, i % 4, i * 128, 1)
                return 0
            lax.fori_loop(0, 16, step, 0)

        pl.run_scoped(norm_phase, pltpu.VMEM((4, 2, 128, HD), BF), pltpu.SemaphoreType.DMA((4, 2)))

        def ustore(n):
            return pltpu.make_async_copy(obuf.at[n % 2, :, pl.ds(0, FW)], ubuf.at[:, pl.ds(pl.multiple_of((n - F0) * FW, FW), FW)], ol.at[n % 2])

        def gate_step(n, _):
            item(n + YAHEAD + 3, 'ysend', 'FG')
            item(n + 6, 'yf', 'FG')
            item(n + 4, 'xf', 'FG')
            item(n + 3, 'done', 'FG')
            load(n + 3, 'F')

            @pl.when(n >= F0 + 2)
            def _():
                ustore(n - 2).wait()
            loaded(n, 'F')
            slot = n % SLOTS

            def mt(t, _):
                rows = pl.ds(pl.multiple_of(t * MT, MT), MT)
                acc = project(rows, slot)
                gate, up = acc[:, :FW], acc[:, FW:]
                obuf[n % 2, rows, pl.ds(0, FW)] = (gate * jax.nn.sigmoid(gate) * up).astype(BF)
                return 0
            lax.fori_loop(0, TOK // MT, mt, 0)
            ustore(n).start()
            return 0
        lax.fori_loop(F0, G0, gate_step, 0)
        for n in (G0 - 2, G0 - 1):
            ustore(jnp.int32(n)).wait()

    pl.run_scoped(scope, pltpu.VMEM((2, TOK, HD), BF), pltpu.VMEM((SLOTS, 2, HD, CW), BF), pltpu.VMEM((2, TOK, CW), BF),
                  pltpu.SemaphoreType.DMA((SLOTS, 4)), pltpu.SemaphoreType.DMA((2,)))

    MD = 512

    def down_phase(u, wbuf, hb, yb, ul, wl, hl, yl):
        def ucopy(t):
            rows = pl.ds(t * MD, MD)
            return pltpu.make_async_copy(ubuf.at[rows], u.at[rows], ul.at[t])

        def wcopies(n):
            cols = pl.ds(pl.multiple_of((n - G0) * FW, FW), FW)
            return [pltpu.make_async_copy(b.at[:, cols], wbuf.at[n % 2, pl.ds(pl.multiple_of(h * HF, 128), HF)], wl.at[n % 2, i])
                    for i, (b, h) in enumerate(((wd, f), (rd, 1 - f)))]

        tiles = TOK // MD

        def at(q):
            return pl.ds(pl.multiple_of((q % tiles) * MD, MD), MD), pl.ds(pl.multiple_of((q // tiles) * FW, FW), FW)

        def hcopy(q):
            return pltpu.make_async_copy(hbuf.at[at(q)], hb.at[q % 2], hl.at[q % 2])

        def ycopy(q):
            return pltpu.make_async_copy(yb.at[q % 2], y.at[at(q)], yl.at[q % 2])

        for t in range(TOK // MD):
            ucopy(t).start()
            if t == 0:
                for c in wcopies(jnp.int32(G0)):
                    c.start()
                hcopy(jnp.int32(0)).start()

        def step(n, _):
            item(n + YAHEAD + 3, 'ysend', 'G')

            @pl.when(n + 3 >= G0 + 6)
            def _():
                item(n + 3, 'yf', 'G')

            @pl.when(n + 2 >= G0 + 4)
            def _():
                item(n + 2, 'xf', 'G')

            @pl.when(n + 1 >= G0 + 3)
            def _():
                item(n + 1, 'done', 'G')

            @pl.when(n + 1 < N)
            def _():
                for c in wcopies(n + 1):
                    c.start()
            for c in wcopies(n):
                c.wait()

            def mt(t, _):
                rows = pl.ds(pl.multiple_of(t * MD, MD), MD)
                q = (n - G0) * tiles + t

                @pl.when(n == G0)
                def _():
                    pltpu.make_async_copy(ubuf.at[rows], u.at[rows], ul.at[t]).wait()

                @pl.when(q + 1 < NG * tiles)
                def _():
                    hcopy(q + 1).start()

                @pl.when(q >= 2)
                def _():
                    ycopy(q - 2).wait()
                hcopy(q).wait()
                acc = None
                for a, b in KSPLIT:
                    part = jnp.dot(u[rows, a:b], wbuf[n % 2, a:b], preferred_element_type=F32)
                    acc = part if acc is None else acc + part
                yb[q % 2] = (hb[q % 2].astype(F32) + acc).astype(BF)
                ycopy(q).start()
                return 0
            lax.fori_loop(0, tiles, mt, 0)
            return 0
        lax.fori_loop(G0, N, step, 0)
        for q in (NG * tiles - 2, NG * tiles - 1):
            ycopy(jnp.int32(q)).wait()

    pl.run_scoped(down_phase, pltpu.VMEM((TOK, FFN), BF), pltpu.VMEM((2, FFN, FW), BF), pltpu.VMEM((2, MD, FW), BF), pltpu.VMEM((2, MD, FW), BF),
                  pltpu.SemaphoreType.DMA((TOK // MD,)), pltpu.SemaphoreType.DMA((2, 2)), pltpu.SemaphoreType.DMA((2,)), pltpu.SemaphoreType.DMA((2,)))


def local_layer(x_loc, norm_attn, w_query, w_key, w_value, w_out, norm_mlp, w_gate, w_up, w_down):
    shape = x_loc.shape
    x2 = x_loc.reshape(TOK, D)
    gains = jnp.stack([norm_attn, norm_mlp]).astype(F32)
    idx = jnp.arange(512, dtype=jnp.int32)
    pos = (idx % 128) * 4 + idx // 128
    inv_freq = jnp.exp(jnp.arange(HEAD // 2, dtype=F32) * (-2.0 * math.log(THETA) / HEAD))
    ang = pos.astype(F32)[:, None] * inv_freq[None, :]
    cos, sin = jnp.cos(ang), jnp.sin(ang)
    cos = jnp.concatenate([cos, cos], axis=1)
    sin = jnp.concatenate([-sin, sin], axis=1)
    qpos = jnp.broadcast_to(pos[:, None], (512, 128))
    kpos = pos[None, :]
    anys = pl.BlockSpec(memory_space=pl.ANY)
    vm = pl.BlockSpec(memory_space=pltpu.VMEM)

    def out(*sh):
        return jax.ShapeDtypeStruct(sh, BF)
    sem = pltpu.SemaphoreType.DMA
    res = pl.pallas_call(
        kernel,
        out_shape=[out(TOK, D), out(TOK, D), out(HD, D), out(HD, D), out(HD, D), out(HD, D), out(HD, FFN), out(HD, FFN), out(HF, D),
                   out(TOK, D), out(TOK, FFN), out(TOK, D)],
        in_specs=[anys, vm, vm, vm, vm, vm] + [anys] * 7,
        out_specs=[anys] * 12,
        scratch_shapes=[pltpu.VMEM((2, HD), F32)] + [sem((NSEM,))] * 8 + [sem((2,)), sem((4, 3)), sem((4, 3)), sem((8, 3)), sem((8, 3))],
        compiler_params=pltpu.CompilerParams(collective_id=0, has_side_effects=True, vmem_limit_bytes=66_900_000),
        cost_estimate=pl.CostEstimate(flops=846 * 10**9, bytes_accessed=10**9, transcendentals=0),
        name='layer',
    )(x2, gains, cos, sin, qpos, kpos, w_query, w_key, w_value, w_out, w_gate, w_up, w_down)
    return res[0].reshape(shape)


def solution(mesh):
    rows = P(('dp', 'fsdp'), 'sp', None)
    weight = P('fsdp', None)
    gain = P('fsdp')
    specs = (rows, gain, weight, weight, weight, weight, gain, weight, weight, weight)
    return jax.shard_map(local_layer, mesh=mesh, in_specs=specs, out_specs=rows, check_vma=False)
```

time: 5660 us -> 1460 us (0.26)
  waiting for transfers between devices: 4040 us -> 0 us
  Pallas kernels: 0 us -> 1440 us
  matrix products: 1110 us -> 0 us
  other arithmetic: 325 us -> 3.24 us
  local copies, waits for them, and re-layouts: 161 us -> 16.3 us
    all_gather x9 -> x0, waiting for transfers between devices: 4030 us -> none  [the longest x7 3570 us: gather_weight(): return lax.all_gather(weight_shard, 'fsdp', axis=0, tiled=True)]
    pallas_call x0 -> x1, Pallas kernels: none -> 1440 us  [local_layer(): pl.pallas_call(kernel, out_shape=[out(TOK, D), out(TOK, D), out(HD, D), o...]
    dot_general x9 -> x0, matrix products: 1110 us -> none  [the longest x1 224 us: local_layer(): jnp.dot(hidden_mlp, gather_weight(w_down), preferred_element_type=jnp.flo...]
    another operation x1 -> x0, other arithmetic: 164 us -> none
    sub x1 -> x0, other arithmetic: 132 us -> none  [local_layer(): jax.nn.softmax(jnp.where(allowed, scores, MASK_VALUE), axis=-1)]
    slice x1 -> x0, local copies, waits for them, and re-layouts: 84.2 us -> none  [apply_rope(): lower_half = proj[..., :half_dim]]
  transfers between devices with their start and end apart: 9 -> 0, of which waited for: 9 -> 0; matrix products, arithmetic and copies ran while one was open for 24% -> 0% of each run, Pallas kernels for 0% -> 0%
where the time goes in v1:
time: 1460 us
  Pallas kernels  1440 us (99%)
  local copies, waits for them, and re-layouts  16.3 us (1%)
    pallas_call x1, Pallas kernels, local_layer(): pl.pallas_call(kernel, out_shape=[out(TOK, D), out(TOK, D), out(HD, D), o...  1440 us

profile of v1, /device:TPU:0, one launch (start us, length us, event | category | flops | bytes accessed | tf_op | source)
XLA Modules:
  0.0 1460.6 jit_solution(105440713970471617)
XLA Ops:
  0.0 0.6 fusion.6.kpos
  0.6 0.7 stack.9
  1.3 0.7 stack.10
  2.0 0.6 maximum_convert_fusion.gown
  2.6 0.8 broadcast_in_dim.2.qpos
  3.5 1.0 fusion
  4.5 1.0 pad_maximum_fusion
  5.5 1441.0 %layer.1 = (bf16[2048,4096]{1,0:T(8,128)(2,1)}, bf16[2048,4096]{1,0:T(8,128)(2,1)}, bf16[2048,4096]{1,0:T(8,128)(2,1)}, bf16[2048,4096]{1,0:T(8,128)(2,1)}, bf16...) custom-call(bf16[2048,4096]{1,0:T(8,128)(2,1)} %bitcast.3, ...), custom_call_target="tpu_custom_call" | custom-call | flops 846000029696 | bytes 1000000000 | tf_op jit(solution)/shard_map/layer/pallas_call | solution.py:550
  1446.5 14.1 copy.12
  (3 shorter events, 0.0 us)

commit v2 on v1

--- a/solution.py
+++ b/solution.py
@@ -30,16 +30,19 @@
 N = G0 + NG
 NSEM = NC + NE + 2 * NF + NG
 DIRECT = 7
-C_E, C_M = 256, 512
-YAHEAD = 12
+C_E = 352
+E_E = 512
+F_E = 512
+G_E = 1216
+YAHEAD = 14
 SLOTS = 6
 KB = 1024
 KSPLIT = ((0, 2816), (2816, 5632), (5632, 8448), (8448, FFN))
 
 
-def kernel(x_in, gown, cos, sin, qpos, kpos, wq, wk, wv, wo, wg, wu, wd,
+def kernel(x_in, gattn, gmlp, wq, wk, wv, wo, wg, wu, wd,
            y, xr, rq, rk, rv, ro, rg, ru, rd, ob, ubuf, hbuf,
-           grem, ys, yr, xs, xrs, dys, dyr, dxs, dxr, gsem, xsend, xrecv, osend, orecv):
+           gown, grem, gains, cos, sin, qpos, ys, yr, xs, xrs, dys, dyr, dxs, dxr, gsem, xsend, xrecv, osend, orecv):
     f = lax.axis_index('fsdp')
     s = lax.axis_index('sp')
     cx = s // 2
@@ -64,12 +67,12 @@
         return pltpu.make_async_remote_copy(src_ref=src, dst_ref=dst, send_sem=ssem, recv_sem=rsem, device_id=dev, device_id_type=MESH)
 
     class Part:
-        def __init__(self, w, r, col, ncol, half, e, m, sem):
-            self.w, self.r, self.half, self.e, self.m, self.sem = w, r, half, e, m, sem
+        def __init__(self, w, r, col, ncol, half, e, sem):
+            self.w, self.r, self.half, self.e, self.m, self.sem = w, r, half, e, half - 2 * e, sem
             self.cols = pl.ds(col, ncol)
 
         def rows(self, off, n):
-            return pl.ds(pl.multiple_of(cc * self.half + off, 32), n)
+            return pl.ds(pl.multiple_of(cc * self.half + off, 16), n)
 
         def ycopy(self):
             a = (self.rows(cx * self.e, self.e + self.m), self.cols)
@@ -129,19 +132,21 @@
             for j, (w, r) in enumerate(((wq, rq), (wk, rk), (wv, rv))):
                 col = al((n // 3) * CW, CW)
                 if 'D' in cand:
-                    when((n < DIRECT) & (n % 3 == j), lambda: getattr(Part(w, r, col, CW, HD // 2, 0, HD // 2, n), what)())
-                when((n >= DIRECT) & (n < E0) & (n % 3 == j), lambda: getattr(Part(w, r, col, CW, HD // 2, C_E, C_M, n), what)())
+                    when((n < DIRECT) & (n % 3 == j), lambda: getattr(Part(w, r, col, CW, HD // 2, 0, n), what)())
+                when((n >= DIRECT) & (n < E0) & (n % 3 == j), lambda: getattr(Part(w, r, col, CW, HD // 2, C_E, n), what)())
         if 'E' in cand:
-            when((n >= E0) & (n < F0), lambda: getattr(Part(wo, ro, al((n - E0) * CW, CW), CW, HD // 2, HD // 4, 0, n), what)())
+            when((n >= E0) & (n < F0), lambda: getattr(Part(wo, ro, al((n - E0) * CW, CW), CW, HD // 2, E_E, n), what)())
         if 'F' in cand:
             def both():
                 col = al((n - F0) * FW, FW)
                 for i, (w, r) in enumerate(((wg, rg), (wu, ru))):
-                    getattr(Part(w, r, col, FW, HD // 2, HD // 4, 0, F0 + 2 * (n - F0) + i), what)()
+                    getattr(Part(w, r, col, FW, HD // 2, F_E, F0 + 2 * (n - F0) + i), what)()
             when((n >= F0) & (n < G0), both)
         if 'G' in cand:
-            when((n >= G0) & (n < N), lambda: getattr(Part(wd, rd, al((n - G0) * FW, FW), FW, HF // 2, HF // 4, 0, n + NF), what)())
-
+            when((n >= G0) & (n < N), lambda: getattr(Part(wd, rd, al((n - G0) * FW, FW), FW, HF // 2, G_E, n + NF), what)())
+
+    gown[0] = gattn[...].astype(F32)
+    gown[1] = gmlp[...].astype(F32)
     gcopy = rcopy(gown, grem, gsem.at[0], gsem.at[1], ynbr)
     gcopy.start()
     for n in range(3):
@@ -157,8 +162,29 @@
             xcopy(r, k).start()
     for n in range(3, YAHEAD):
         item(n, 'ysend', 'CD')
+
+    def positions(shape, dim):
+        j = lax.broadcasted_iota(jnp.int32, shape, dim)
+        return (j % 128) * 4 + j // 128
+
+    def table(i, _):
+        rs = pl.ds(pl.multiple_of(i * 128, 128), 128)
+        pos = lax.broadcasted_iota(jnp.int32, (128, HEAD), 0) * 4 + i
+        lane = lax.broadcasted_iota(jnp.int32, (128, HEAD), 1)
+        freq = jnp.exp((lane % (HEAD // 2)).astype(F32) * (-2.0 * math.log(THETA) / HEAD))
+        ang = pos.astype(F32) * freq
+        qpos[rs, :] = pos
+        cos[rs, :] = jnp.cos(ang)
+        sn = jnp.sin(ang)
+        sin[rs, :] = jnp.where(lane < HEAD // 2, -sn, sn)
+        return 0
+    lax.fori_loop(0, 4, table, 0)
     gcopy.wait_recv()
     gcopy.wait_send()
+    for g in range(2):
+        for i, src in enumerate((gown, grem)):
+            v = src[g]
+            gains[2 * g + i] = jnp.concatenate([v[k:k + 1] for k in range(HD // 128)], axis=1)
 
     def scope(act, wbuf, obuf, wl, ol):
         def wcopies(n, cand):
@@ -203,8 +229,8 @@
                 ss = jnp.sum(x0 * x0, axis=-1, keepdims=True) + jnp.sum(x1 * x1, axis=-1, keepdims=True)
                 inv = lax.rsqrt(ss * (1.0 / D) + EPS)
                 ro_ = pl.ds(pl.multiple_of(row + i * 16, 16), 16)
-                act[0, ro_, :] = (xt[t, 0, rs, :].astype(F32) * inv * gown[pl.ds(g, 1), :]).astype(BF)
-                act[1, ro_, :] = (xt[t, 1, rs, :].astype(F32) * inv * grem[pl.ds(g, 1), :]).astype(BF)
+                act[0, ro_, :] = (xt[t, 0, rs, :].astype(F32) * inv * gains[2 * g]).astype(BF)
+                act[1, ro_, :] = (xt[t, 1, rs, :].astype(F32) * inv * gains[2 * g + 1]).astype(BF)
                 return 0
             lax.fori_loop(0, 8, sub, 0)
 
@@ -242,6 +268,11 @@
                 dst = ob.at[pl.ds(pl.multiple_of(s * 512, 512), 512), pl.ds(pl.multiple_of(g * CW, CW), CW)]
                 return rcopy(src, dst, osend.at[g, k - 1], orecv.at[g, k - 1], (0, f, peer(k)))
 
+            def orow(g, k, r):
+                src = obuf.at[g % 2, pl.ds(pl.multiple_of(peer(k) * 512 + r * 128, 128), 128)]
+                dst = ob.at[pl.ds(pl.multiple_of(s * 512 + r * 128, 128), 128), pl.ds(pl.multiple_of(g * CW, CW), CW)]
+                return rcopy(src, dst, osend.at[g, k - 1], orecv.at[g, k - 1], (0, f, peer(k)))
+
             def olocal(g):
                 return pltpu.make_async_copy(obuf.at[g % 2, pl.ds(pl.multiple_of(s * 512, 512), 512)],
                                              ob.at[pl.ds(pl.multiple_of(s * 512, 512), 512), pl.ds(pl.multiple_of(g * CW, CW), CW)], ol.at[g % 2])
@@ -281,7 +312,8 @@
                     hs = pl.ds(pl.multiple_of(h * HEAD, HEAD), HEAD)
                     sc = lax.dot_general(qb[:, hs], kb[:, hs], (((1,), (1,)), ((), ())), preferred_element_type=F32)
                     qp = qpos[...]
-                    sc = jnp.where(jnp.concatenate([qp] * 4, axis=1) >= kpos[...], sc, NEG)
+                    kp = positions((1, 512), 1)
+                    sc = jnp.where(jnp.concatenate([qp] * 4, axis=1) >= kp, sc, NEG)
                     mx = jnp.max(sc, axis=-1, keepdims=True)
                     p = jnp.exp2((sc - mx) * (HEAD ** -0.5 * math.log2(math.e)))
                     tot = jnp.sum(p, axis=-1, keepdims=True)
@@ -292,6 +324,12 @@
                     return 0
                 lax.fori_loop(0, CW // HEAD, head, 0)
 
+                for k in (2, 3, 1):
+                    orow(g, k, r).start()
+
+                @pl.when(r == 3)
+                def _():
+                    olocal(g).start()
                 for qq, (yy, dd) in {0: ((3,), ()), 1: ((4,), (3,)), 2: ((5, 6, 7), (4,)), 3: ((8,), (5,))}.items():
                     @pl.when(q == qq)
                     def _():
@@ -306,16 +344,13 @@
                 def _():
                     n = 3 * g + 3 + r
                     item(n + YAHEAD, 'ysend', 'CEF')
-                    item(n + 3, 'yf', 'CEF')
-                    item(n + 1, 'xf', 'CE')
-                    item(n, 'done', 'CDE')
-                    load(n, 'CE')
-
-                @pl.when(r == 3)
-                def _():
-                    for k in (2, 3, 1):
-                        ocopy(g, k).start()
-                    olocal(g).start()
+
+                    @pl.when(g < 7)
+                    def _():
+                        item(n + 3, 'yf', 'CE')
+                        item(n + 1, 'xf', 'CE')
+                        item(n, 'done', 'CD')
+                        load(n, 'C')
                 return 0
 
             for n in range(3):
@@ -323,6 +358,12 @@
                 item(n, 'done', 'CD')
                 load(n, 'C')
             lax.fori_loop(0, 32, unit, 0)
+            for n in range(E0 + 3, E0 + 6):
+                item(n, 'yf', 'E')
+            for n in range(E0, E0 + 3):
+                item(n + 1, 'xf', 'E')
+                item(n, 'done', 'E')
+                load(n, 'E')
             for g in (6, 7):
                 for k in (1, 2, 3):
                     ocopy(g, k).wait_send()
@@ -361,10 +402,15 @@
 
             def step(n, _):
                 item(n + YAHEAD + 3, 'ysend', 'EF')
-                item(n + 6, 'yf', 'EF')
-                item(n + 4, 'xf', 'EF')
-                item(n + 3, 'done', 'EF')
-                load(n + 3, 'EF')
+                @pl.when(n + 5 >= E0 + 6)
+                def _():
+                    item(n + 5, 'yf', 'EF')
+
+                @pl.when(n + 2 >= E0 + 4)
+                def _():
+                    item(n + 2, 'xf', 'EF')
+                    item(n + 1, 'done', 'EF')
+                    load(n + 1, 'EF')
 
                 @pl.when(n + 1 < F0)
                 def _():
@@ -416,10 +462,10 @@
 
         def gate_step(n, _):
             item(n + YAHEAD + 3, 'ysend', 'FG')
-            item(n + 6, 'yf', 'FG')
-            item(n + 4, 'xf', 'FG')
-            item(n + 3, 'done', 'FG')
-            load(n + 3, 'F')
+            item(n + 5, 'yf', 'FG')
+            item(n + 2, 'xf', 'FG')
+            item(n + 1, 'done', 'FG')
+            load(n + 1, 'F')
 
             @pl.when(n >= F0 + 2)
             def _():
@@ -447,13 +493,13 @@
 
     def down_phase(u, wbuf, hb, yb, ul, wl, hl, yl):
         def ucopy(t):
-            rows = pl.ds(t * MD, MD)
+            rows = pl.ds(pl.multiple_of(t * MD, MD), MD)
             return pltpu.make_async_copy(ubuf.at[rows], u.at[rows], ul.at[t])
 
-        def wcopies(n):
+        def wcopy(n, i):
             cols = pl.ds(pl.multiple_of((n - G0) * FW, FW), FW)
-            return [pltpu.make_async_copy(b.at[:, cols], wbuf.at[n % 2, pl.ds(pl.multiple_of(h * HF, 128), HF)], wl.at[n % 2, i])
-                    for i, (b, h) in enumerate(((wd, f), (rd, 1 - f)))]
+            h = (f, 1 - f)[i]
+            return pltpu.make_async_copy((wd, rd)[i].at[:, cols], wbuf.at[n % 2, pl.ds(pl.multiple_of(h * HF, 128), HF)], wl.at[n % 2, i])
 
         tiles = TOK // MD
 
@@ -466,42 +512,35 @@
         def ycopy(q):
             return pltpu.make_async_copy(yb.at[q % 2], y.at[at(q)], yl.at[q % 2])
 
-        for t in range(TOK // MD):
+        for t in range(tiles):
             ucopy(t).start()
             if t == 0:
-                for c in wcopies(jnp.int32(G0)):
-                    c.start()
+                for i in range(2):
+                    wcopy(jnp.int32(G0), i).start()
                 hcopy(jnp.int32(0)).start()
 
         def step(n, _):
             item(n + YAHEAD + 3, 'ysend', 'G')
 
-            @pl.when(n + 3 >= G0 + 6)
+            @pl.when(n + 4 >= G0 + 5)
             def _():
-                item(n + 3, 'yf', 'G')
-
-            @pl.when(n + 2 >= G0 + 4)
-            def _():
-                item(n + 2, 'xf', 'G')
-
-            @pl.when(n + 1 >= G0 + 3)
-            def _():
-                item(n + 1, 'done', 'G')
+                item(n + 4, 'yf', 'G')
+            item(n + 2, 'xf', 'G')
+            item(n + 1, 'done', 'G')
 
             @pl.when(n + 1 < N)
             def _():
-                for c in wcopies(n + 1):
-                    c.start()
-            for c in wcopies(n):
-                c.wait()
+                for i in range(2):
+                    wcopy(n + 1, i).start()
+            for i in range(2):
+                wcopy(n, i).wait()
 
             def mt(t, _):
-                rows = pl.ds(pl.multiple_of(t * MD, MD), MD)
                 q = (n - G0) * tiles + t
 
                 @pl.when(n == G0)
                 def _():
-                    pltpu.make_async_copy(ubuf.at[rows], u.at[rows], ul.at[t]).wait()
+                    ucopy(t).wait()
 
                 @pl.when(q + 1 < NG * tiles)
                 def _():
@@ -511,6 +550,7 @@
                 def _():
                     ycopy(q - 2).wait()
                 hcopy(q).wait()
+                rows = pl.ds(pl.multiple_of(t * MD, MD), MD)
                 acc = None
                 for a, b in KSPLIT:
                     part = jnp.dot(u[rows, a:b], wbuf[n % 2, a:b], preferred_element_type=F32)
@@ -531,16 +571,6 @@
 def local_layer(x_loc, norm_attn, w_query, w_key, w_value, w_out, norm_mlp, w_gate, w_up, w_down):
     shape = x_loc.shape
     x2 = x_loc.reshape(TOK, D)
-    gains = jnp.stack([norm_attn, norm_mlp]).astype(F32)
-    idx = jnp.arange(512, dtype=jnp.int32)
-    pos = (idx % 128) * 4 + idx // 128
-    inv_freq = jnp.exp(jnp.arange(HEAD // 2, dtype=F32) * (-2.0 * math.log(THETA) / HEAD))
-    ang = pos.astype(F32)[:, None] * inv_freq[None, :]
-    cos, sin = jnp.cos(ang), jnp.sin(ang)
-    cos = jnp.concatenate([cos, cos], axis=1)
-    sin = jnp.concatenate([-sin, sin], axis=1)
-    qpos = jnp.broadcast_to(pos[:, None], (512, 128))
-    kpos = pos[None, :]
     anys = pl.BlockSpec(memory_space=pl.ANY)
     vm = pl.BlockSpec(memory_space=pltpu.VMEM)
 
@@ -551,13 +581,14 @@
         kernel,
         out_shape=[out(TOK, D), out(TOK, D), out(HD, D), out(HD, D), out(HD, D), out(HD, D), out(HD, FFN), out(HD, FFN), out(HF, D),
                    out(TOK, D), out(TOK, FFN), out(TOK, D)],
-        in_specs=[anys, vm, vm, vm, vm, vm] + [anys] * 7,
+        in_specs=[anys, vm, vm] + [anys] * 7,
         out_specs=[anys] * 12,
-        scratch_shapes=[pltpu.VMEM((2, HD), F32)] + [sem((NSEM,))] * 8 + [sem((2,)), sem((4, 3)), sem((4, 3)), sem((8, 3)), sem((8, 3))],
+        scratch_shapes=[pltpu.VMEM((2, HD // 128, 128), F32)] * 2 + [pltpu.VMEM((4, 1, HD), F32)]
+        + [pltpu.VMEM((512, HEAD), F32)] * 2 + [pltpu.VMEM((512, 128), jnp.int32)] + [sem((NSEM,))] * 8 + [sem((2,)), sem((4, 3)), sem((4, 3)), sem((8, 3)), sem((8, 3))],
         compiler_params=pltpu.CompilerParams(collective_id=0, has_side_effects=True, vmem_limit_bytes=66_900_000),
         cost_estimate=pl.CostEstimate(flops=846 * 10**9, bytes_accessed=10**9, transcendentals=0),
         name='layer',
-    )(x2, gains, cos, sin, qpos, kpos, w_query, w_key, w_value, w_out, w_gate, w_up, w_down)
+    )(x2, norm_attn.reshape(HD // 128, 128), norm_mlp.reshape(HD // 128, 128), w_query, w_key, w_value, w_out, w_gate, w_up, w_down)
     return res[0].reshape(shape)
 
 

time: 1460 us -> 1350 us (0.925)
  Pallas kernels: 1440 us -> 1330 us
    pallas_call x1, Pallas kernels: 1440 us -> 1330 us  [local_layer(): pl.pallas_call(kernel, out_shape=[out(TOK, D), out(TOK, D), out(HD, D), o...]
where the time goes in v2:
time: 1350 us
  Pallas kernels  1330 us (99%)
  local copies, waits for them, and re-layouts  14.1 us (1%)
    pallas_call x1, Pallas kernels, local_layer(): pl.pallas_call(kernel, out_shape=[out(TOK, D), out(TOK, D), out(HD, D), o...  1330 us

profile of v2, /device:TPU:0, one launch (start us, length us, event | category | flops | bytes accessed | tf_op | source)
XLA Modules:
  0.0 1348.3 jit_solution(7361599716933588254)
XLA Ops:
  0.0 1334.3 %layer.1 = (bf16[2048,4096]{1,0:T(8,128)(2,1)}, bf16[2048,4096]{1,0:T(8,128)(2,1)}, bf16[2048,4096]{1,0:T(8,128)(2,1)}, bf16[2048,4096]{1,0:T(8,128)(2,1)}, bf16...) custom-call(bf16[2048,4096]{1,0:T(8,128)(2,1)} %bitcast.5, ...), custom_call_target="tpu_custom_call" | custom-call | flops 846000029696 | bytes 1000000000 | tf_op jit(solution)/shard_map/layer/pallas_call | solution.py:580
  1334.3 14.1 %copy.12 = bf16[16,128,4096]{2,1,0:T(8,128)(2,1)} copy(bf16[16,128,4096]{2,1,0:T(8,128)(2,1)} %bitcast.4) | data formatting | bytes 33554432

commit v3 on v0

v3 whole, which is shorter than its diff:
```python
import math
import functools
import jax
import jax.numpy as jnp
from jax import lax
from jax.experimental import pallas as pl
from jax.experimental.pallas import tpu as pltpu
from jax.sharding import PartitionSpec as P

HEAD = 128
LN = HEAD
SEQ = 512
EPS = 1e-5
THETA = 5e7
NEG = -1e30
BF = jnp.bfloat16
F32 = jnp.float32
MESH = pl.DeviceIdType.MESH

D = 4096
HD = D // 2
FFN = 11008
HF = FFN // 2
TOK = 2048
GW = 256
CW = 512
FW = 256
ROWS = 8

NC, NE, NF, NG = 8, 8, 43, 16
E0 = NC
F0 = E0 + NE
G0 = F0 + NF
N = G0 + NG
YR, XR = 64, 32
FD = F0 + 3
F_E = 512
G_E = 1360
YAHEAD = 16
SLOTS = 2
KB = 1024
KSPLIT = ((0, 2816), (2816, 5632), (5632, 8448), (8448, FFN))
MT = 1024
NB = 64
MD = 512


def kernel(x_in, gattn, gmlp, wq, wk, wv, wo, wg, wu, wd,
           y, xr, rq, rk, rv, ro, rg, ru, rd, ob, ostage, psum, ubuf, hbuf,
           gown, grem, gains, cos, sin, qpos, ys, yr, xs, xrs, dys, dyr, dxs, dxr, gsem, xsend, xrecv, osend, orecv):
    f = lax.axis_index('fsdp')
    s = lax.axis_index('sp')
    cx = s // 2
    cc = s % 2
    ynbr = (0, 1 - f, s)
    xnbr = (0, f, (s + 2) % 4)
    pnbr = (0, f, cx * 2 + 1 - cc)

    def peer(k):
        if k == 1:
            return cx * 2 + 1 - cc
        if k == 2:
            return (s + 2) % 4
        return 3 - s

    bar = pltpu.get_barrier_semaphore()
    for dev in (ynbr, pnbr, xnbr, (0, f, 3 - s)):
        pl.semaphore_signal(bar, inc=1, device_id=dev, device_id_type=MESH)
    pl.semaphore_wait(bar, 4)

    def rcopy(src, dst, ssem, rsem, dev):
        return pltpu.make_async_remote_copy(src_ref=src, dst_ref=dst, send_sem=ssem, recv_sem=rsem, device_id=dev, device_id_type=MESH)

    class Part:
        def __init__(self, w, r, col, ncol, half, e, sem):
            self.w, self.r, self.half, self.e, self.m = w, r, half, e, half - 2 * e
            self.ysem, self.sem = sem % YR, sem % XR
            self.cols = pl.ds(col, ncol)

        def rows(self, off, n):
            return pl.ds(pl.multiple_of(cc * self.half + off, 16), n)

        def ycopy(self):
            a = (self.rows(cx * self.e, self.e + self.m), self.cols)
            return rcopy(self.w.at[a], self.r.at[a], ys.at[self.ysem], yr.at[self.ysem], ynbr)

        def xcopy(self):
            a = (self.rows(cx * (self.e + self.m), self.e), self.cols)
            return rcopy(self.r.at[a], self.r.at[a], xs.at[self.sem], xrs.at[self.sem], xnbr)

        def dycopy(self):
            a = (self.rows(cx * self.e, self.e + self.m), self.cols)
            return rcopy(self.r.at[a], self.r.at[a], dys.at[self.sem], dyr.at[self.sem], pnbr)

        def dxcopy(self):
            a = (self.rows((1 - cx) * (self.e + self.m), self.e), self.cols)
            return rcopy(self.r.at[a], self.r.at[a], dxs.at[self.sem], dxr.at[self.sem], pnbr)

        def ysend(self):
            self.ycopy().start()

        def yf(self):
            c = self.ycopy()
            c.wait_recv()
            if self.e:
                self.xcopy().start()
            self.dycopy().start()
            c.wait_send()

        def xf(self):
            if self.e:
                c = self.xcopy()
                c.wait_recv()
                self.dxcopy().start()
                c.wait_send()

        def done(self):
            c = self.dycopy()
            c.wait_recv()
            c.wait_send()
            if self.e:
                c = self.dxcopy()
                c.wait_recv()
                c.wait_send()

    def al(v, k):
        return v if isinstance(v, int) else pl.multiple_of(v, k)

    def when(cond, fn):
        if isinstance(cond, bool):
            if cond:
                fn()
        else:
            pl.when(cond)(fn)

    def item(n, what, cand):
        def run(pairs, col, ncol, half, e, sem):
            for i, (w, r) in enumerate(pairs):
                getattr(Part(w, r, col, ncol, half, e, sem + i), what)()

        if 'C' in cand:
            when(n < E0, lambda: run(((wq, rq), (wk, rk), (wv, rv)), pl.multiple_of(cx * HD + n * GW, GW), GW, HD // 2, 0, 3 * n))
        if 'E' in cand:
            when((n >= E0) & (n < F0), lambda: run(((wo, ro),), al((n - E0) * CW, CW), CW, HD // 2, 0, n + 2 * NC))
        if 'F' in cand:
            pairs = ((wg, rg), (wu, ru))
            if 'D' in cand:
                when((n >= F0) & (n < FD), lambda: run(pairs, al((n - F0) * FW, FW), FW, HD // 2, 0, 2 * n + 2 * NC - F0))
            when((n >= FD) & (n < G0), lambda: run(pairs, al((n - F0) * FW, FW), FW, HD // 2, F_E, 2 * n + 2 * NC - F0))
        if 'W' in cand or 'G' in cand:
            when((n >= G0) & (n < N - 1), lambda: run(((wd, rd),), al((n - G0) * FW, FW), FW, HF // 2, G_E, n + 2 * NC + NF))
        if 'G' in cand:
            when(n == N - 1, lambda: run(((wd, rd),), D - FW, FW, HF // 2, 0, n + 2 * NC + NF))

    gown[0] = gattn[...].astype(F32)
    gown[1] = gmlp[...].astype(F32)
    gcopy = rcopy(gown, grem, gsem.at[0], gsem.at[1], ynbr)
    gcopy.start()
    item(0, 'ysend', 'C')

    def xcopy(r, k):
        first = (cc if k == 2 else 1 - cc) * ROWS
        src = x_in.at[pl.ds(pl.multiple_of((first + r) * LN, LN), LN)]
        dst = xr.at[pl.ds(pl.multiple_of(r * SEQ + s * LN, LN), LN)]
        return rcopy(src, dst, xsend.at[r, k - 1], xrecv.at[r, k - 1], (0, f, peer(k)))

    for r in range(ROWS):
        for k in (2, 3, 1):
            xcopy(r, k).start()
    for n in range(1, 4):
        item(n, 'ysend', 'C')

    def positions(shape, dim):
        j = lax.broadcasted_iota(jnp.int32, shape, dim)
        return (j % LN) * 4 + j // LN

    def table(i, _):
        rs = pl.ds(pl.multiple_of(i * LN, LN), LN)
        pos = lax.broadcasted_iota(jnp.int32, (LN, HEAD), 0) * 4 + i
        lane = lax.broadcasted_iota(jnp.int32, (LN, HEAD), 1)
        freq = jnp.exp((lane % (HEAD // 2)).astype(F32) * (-2.0 * math.log(THETA) / HEAD))
        ang = pos.astype(F32) * freq
        qpos[rs, :] = pos
        cos[rs, :] = jnp.cos(ang)
        sn = jnp.sin(ang)
        sin[rs, :] = jnp.where(lane < HEAD // 2, -sn, sn)
        return 0
    lax.fori_loop(0, 4, table, 0)
    gcopy.wait_recv()
    gcopy.wait_send()
    for g in range(2):
        for i, src in enumerate((gown, grem)):
            v = src[g]
            gains[2 * g + i] = jnp.concatenate([v[k:k + 1] for k in range(HD // LN)], axis=1)

    def norm_tile(act, xt, t, row, g):
        def sub(i, _):
            for o in range(0, NB, 16):
                rs = pl.ds(pl.multiple_of(i * NB + o, 16), 16)
                x0 = xt[t, 0, rs, :].astype(F32)
                x1 = xt[t, 1, rs, :].astype(F32)
                ss = jnp.sum(x0 * x0, axis=-1, keepdims=True) + jnp.sum(x1 * x1, axis=-1, keepdims=True)
                inv = lax.rsqrt(ss * (1.0 / D) + EPS)
                to = pl.ds(pl.multiple_of(row + i * NB + o, 16), 16)
                act[0, to, :] = (xt[t, 0, rs, :].astype(F32) * inv * gains[2 * g]).astype(BF)
                act[1, to, :] = (xt[t, 1, rs, :].astype(F32) * inv * gains[2 * g + 1]).astype(BF)
            return 0
        lax.fori_loop(0, LN // NB, sub, 0)

    def halves(src, row, xt, t, sem):
        rows = pl.ds(row, LN)
        return [pltpu.make_async_copy(src.at[rows, pl.ds(pl.multiple_of(h * HD, HD), HD)], xt.at[t, i], sem.at[t, i])
                for i, h in enumerate((f, 1 - f))]

    def product(act, rows, wbuf, slot):
        acc = None
        for i in range(2):
            for k in range(0, HD, KB):
                part = jnp.dot(act[i, rows, k:k + KB], wbuf[slot, i, k:k + KB], preferred_element_type=F32)
                acc = part if acc is None else acc + part
        return acc

    def oremote(k):
        first = cc * ROWS * LN
        return rcopy(ostage.at[k - 1], ob.at[pl.ds(pl.multiple_of(first, LN), ROWS * LN), pl.ds(pl.multiple_of(cx * HD, HD), HD)],
                     osend.at[k - 1], orecv.at[k - 1], (0, f, peer(k)))

    def attention_phase(act, wbuf, obuf, xt, qb, kb, vb, wl, ol, xl):
        def wcopies(j, slot):
            cols = pl.ds(pl.multiple_of(cx * HD + j * GW, GW), GW)
            return [pltpu.make_async_copy(b.at[:, cols], wbuf.at[slot, i, :, pl.ds(t * GW, GW)], wl.at[slot, i, t])
                    for t, pair in enumerate(((wq, rq), (wk, rk), (wv, rv))) for i, b in enumerate(pair)]

        def tokens(r):
            for k in (1, 2, 3):
                c = xcopy(r, k)
                c.wait_recv()
                c.wait_send()

            def cps(t):
                return halves(xr, pl.multiple_of(r * SEQ + t * LN, LN), xt, t, xl)
            for t in range(4):
                @pl.when(s != t)
                def _():
                    for c in cps(t):
                        c.start()

                @pl.when(s == t)
                def _():
                    for c in halves(x_in, pl.multiple_of((cc * ROWS + r) * LN, LN), xt, t, xl):
                        c.start()
            for t in range(4):
                for c in cps(t):
                    c.wait()
                norm_tile(act, xt, t, r * SEQ + t * LN, 0)

        def rope(u):
            out = []
            for h in range(GW // HEAD):
                v = u[:, h * HEAD:(h + 1) * HEAD]
                out.append(v * cos[...] + pltpu.roll(v, HEAD // 2, 1) * sin[...])
            return jnp.concatenate(out, axis=1).astype(BF)

        def place(r, j):
            return (pl.ds(pl.multiple_of((cc * ROWS + r) * LN, LN), LN), pl.ds(pl.multiple_of(cx * HD + j * GW, GW), GW))

        def stage(r, j, k):
            return ostage.at[k - 1, pl.ds(pl.multiple_of(r * LN, LN), LN), pl.ds(pl.multiple_of(j * GW, GW), GW)]

        def ostore(r, j, slot):
            own = pltpu.make_async_copy(obuf.at[slot, pl.ds(pl.multiple_of(s * LN, LN), LN)], ob.at[place(r, j)], ol.at[slot, 0])
            return [own] + [pltpu.make_async_copy(obuf.at[slot, pl.ds(pl.multiple_of(peer(k) * LN, LN), LN)], stage(r, j, k), ol.at[slot, k])
                            for k in (1, 2, 3)]

        def osends(r, j, slot):
            for c in ostore(r, j, slot):
                c.wait()
            for k in (2, 3, 1):
                rcopy(stage(r, j, k), ob.at[place(r, j)], osend.at[k - 1], orecv.at[k - 1], (0, f, peer(k))).start()

        def shell(k, _):
            def unit(i, _):
                r = jnp.minimum(i, k)
                j = jnp.minimum(k, 2 * k - i)
                u = k * k + i
                slot = (k * (k + 1) // 2 + k - j) % 2

                def next_group():
                    item(k + 1, 'done', 'C')
                    for c in wcopies(k + 1, 1 - slot):
                        c.start()

                @pl.when(i == k)
                def _():
                    tokens(k)

                    @pl.when((k > 0) & (k < NC - 1))
                    def _():
                        item(k + 1, 'yf', 'C')

                @pl.when((i == 0) | (i > k))
                def _():
                    for c in wcopies(j, slot):
                        c.wait()

                    @pl.when(j > 0)
                    def _():
                        for c in wcopies(j - 1, 1 - slot):
                            c.start()

                    @pl.when((j == 0) & (k > 0) & (k < NC - 1))
                    def _():
                        next_group()

                rows = pl.ds(pl.multiple_of(r * SEQ, SEQ), SEQ)
                acc = product(act, rows, wbuf, slot)
                qb[...] = rope(acc[:, :GW])
                kb[...] = rope(acc[:, GW:2 * GW])
                vb[...] = acc[:, 2 * GW:].astype(BF)

                def head(h, _):
                    hs = pl.ds(pl.multiple_of(h * HEAD, HEAD), HEAD)
                    sc = lax.dot_general(qb[:, hs], kb[:, hs], (((1,), (1,)), ((), ())), preferred_element_type=F32)
                    qp = qpos[...]
                    kp = positions((1, SEQ), 1)
                    sc = jnp.where(jnp.concatenate([qp] * 4, axis=1) >= kp, sc, NEG)
                    mx = jnp.max(sc, axis=-1, keepdims=True)
                    p = jnp.exp2((sc - mx) * (HEAD ** -0.5 * math.log2(math.e)))
                    tot = jnp.sum(p, axis=-1, keepdims=True)
                    o = jnp.dot(p.astype(BF), vb[:, hs], preferred_element_type=F32) / tot
                    obuf[u % 2, :, hs] = o.astype(BF)
                    return 0
                lax.fori_loop(0, GW // HEAD, head, 0)
                for c in ostore(r, j, u % 2):
                    c.start()

                @pl.when(i > 0)
                def _():
                    osends(jnp.minimum(i - 1, k), jnp.minimum(k, 2 * k - i + 1), (u + 1) % 2)

                @pl.when((i == 0) & (k > 0))
                def _():
                    osends(k - 1, 0, (u + 1) % 2)

                @pl.when(u % 4 == 0)
                def _():
                    item(u // 4 + 4, 'ysend', 'CEFD')

                @pl.when(k == 0)
                def _():
                    item(1, 'yf', 'C')
                    next_group()
                return 0
            lax.fori_loop(0, 2 * k + 1, unit, 0)
            return 0

        item(0, 'yf', 'C')
        item(0, 'done', 'C')
        for c in wcopies(jnp.int32(0), jnp.int32(0)):
            c.start()
        lax.fori_loop(0, NC, shell, 0)
        osends(jnp.int32(ROWS - 1), jnp.int32(0), jnp.int32((NC * NC - 1) % 2))

    pl.run_scoped(attention_phase, pltpu.VMEM((2, ROWS * SEQ, HD), BF), pltpu.VMEM((2, 2, HD, 3 * GW), BF), pltpu.VMEM((2, SEQ, GW), BF),
                  pltpu.VMEM((4, 2, LN, HD), BF), pltpu.VMEM((SEQ, GW), BF), pltpu.VMEM((SEQ, GW), BF), pltpu.VMEM((SEQ, GW), BF),
                  pltpu.SemaphoreType.DMA((2, 2, 3)), pltpu.SemaphoreType.DMA((2, 4)), pltpu.SemaphoreType.DMA((4, 2)))

    for n in range(E0, F0):
        item(n, 'yf', 'E')
    for n in range(20, 24):
        item(n, 'ysend', 'FD')

    def dcopy(wdown, dl, n, i):
        cols = pl.ds(pl.multiple_of((n - G0) * FW, FW), FW)
        h = (f, 1 - f)[i]
        return pltpu.make_async_copy((wd, rd)[i].at[:, cols], wdown.at[n % 2, pl.ds(pl.multiple_of(h * HF, LN), HF)], dl.at[n % 2, i])

    def scope(wdown, dl, act, wbuf, obuf, wl, ol):
        def wcopies(n, cand):
            def go(fn):
                slot = n % SLOTS
                if 'F' in cand:
                    def ff():
                        cols = pl.ds(al((n - F0) * FW, FW), FW)
                        for i, pair in enumerate(((wg, wu), (rg, ru))):
                            for j, b in enumerate(pair):
                                fn(pltpu.make_async_copy(b.at[:, cols], wbuf.at[slot, i, :, pl.ds(j * FW, FW)], wl.at[slot, i + 2 * j]))
                    when((n >= F0) & (n < G0), ff)
            return go

        def load(n, cand):
            wcopies(n, cand)(lambda c: c.start())

        def loaded(n, cand):
            wcopies(n, cand)(lambda c: c.wait())

        def out_phase(hx, pb, hl, pp, al_):
            def ecopy(n, i):
                h = cx if i == 0 else 1 - cx
                cols = pl.ds(al((n - E0) * CW, CW), CW)
                return h, lambda w: pltpu.make_async_copy(w.at[:, cols], wbuf.at[n % SLOTS, i], wl.at[n % SLOTS, i])

            def eload(n, i):
                h, copy = ecopy(n, i)
                pl.when(h == f)(lambda: copy(wo).start())
                pl.when(h != f)(lambda: copy(ro).start())

            def eloaded(n, i):
                ecopy(n, i)[1](wo).wait()

            def acopy(t, i):
                h = cx if i == 0 else 1 - cx
                rows = pl.ds(t * MT, MT)
                return pltpu.make_async_copy(ob.at[rows, pl.ds(pl.multiple_of(h * HD, HD), HD)], act.at[i, rows], al_.at[t, i])

            def cols(n):
                return pl.ds(pl.multiple_of((n - E0) * CW, CW), CW)

            def xload(n):
                return pltpu.make_async_copy(x_in.at[:, cols(n)], hx.at[n % 2], hl.at[n % 2])

            def pstore(n):
                return pltpu.make_async_copy(pb.at[n % 2], psum.at[:, cols(n)], pp.at[0, n % 2])

            def pload(n):
                return pltpu.make_async_copy(psum.at[:, cols(n)], pb.at[n % 2], pp.at[1, n % 2])

            def hstore(n):
                return pltpu.make_async_copy(obuf.at[n % 2], hbuf.at[:, cols(n)], ol.at[n % 2])

            def eproduct(rows, slot, i):
                acc = None
                for k in range(0, HD, KB):
                    part = jnp.dot(act[i, rows, k:k + KB], wbuf[slot, i, k:k + KB], preferred_element_type=F32)
                    acc = part if acc is None else acc + part
                return acc

            first = jnp.int32(E0)
            item(E0, 'done', 'E')
            eload(first, 0)
            xload(first).start()
            c = oremote(1)
            c.wait_recv()
            c.wait_send()
            for t in range(TOK // MT):
                acopy(t, 0).start()
            for t in range(TOK // MT):
                acopy(t, 0).wait()

            def step1(n, _):
                @pl.when(n + 1 < F0)
                def _():
                    item(n + 1, 'done', 'E')
                    eload(n + 1, 0)
                    xload(n + 1).start()

                @pl.when(n >= E0 + 2)
                def _():
                    pstore(n - 2).wait()
                eloaded(n, 0)
                xload(n).wait()

                def mt(t, _):
                    rows = pl.ds(pl.multiple_of(t * MT, MT), MT)
                    pb[n % 2, rows, :] = hx[n % 2, rows, :].astype(F32) + eproduct(rows, n % SLOTS, 0)
                    return 0
                lax.fori_loop(0, TOK // MT, mt, 0)
                pstore(n).start()
                return 0
            lax.fori_loop(E0, F0, step1, 0)
            for n in (F0 - 2, F0 - 1):
                pstore(jnp.int32(n)).wait()
            eload(first, 1)
            pload(first).start()

            for n in range(F0, FD + 1):
                item(n, 'yf', 'FD')
            for k in (2, 3):
                c = oremote(k)
                c.wait_recv()
                c.wait_send()
            for t in range(TOK // MT):
                acopy(t, 1).start()
            for t in range(TOK // MT):
                acopy(t, 1).wait()

            def step2(n, _):
                item(n + YAHEAD, 'ysend', 'F')

                @pl.when((n == E0) | ((n - E0) * 2 // 5 > (n - E0 - 1) * 2 // 5))
                def _():
                    item(FD + 1 + (n - E0) * 2 // 5, 'yf', 'F')

                @pl.when(n + 1 < F0)
                def _():
                    eload(n + 1, 1)
                    pload(n + 1).start()

                @pl.when(n + 1 == F0)
                def _():
                    item(n + 1, 'done', 'FD')
                    load(n + 1, 'F')

                @pl.when(n >= E0 + 2)
                def _():
                    hstore(n - 2).wait()
                eloaded(n, 1)
                pload(n).wait()

                def mt(t, _):
                    rows = pl.ds(pl.multiple_of(t * MT, MT), MT)
                    obuf[n % 2, rows, :] = (pb[n % 2, rows, :] + eproduct(rows, n % SLOTS, 1)).astype(BF)
                    return 0
                lax.fori_loop(0, TOK // MT, mt, 0)
                hstore(n).start()
                return 0
            lax.fori_loop(E0, F0, step2, 0)
            for n in (F0 - 2, F0 - 1):
                hstore(jnp.int32(n)).wait()

        pl.run_scoped(out_phase, pltpu.VMEM((2, TOK, CW), BF), pltpu.VMEM((2, TOK, CW), F32), pltpu.SemaphoreType.DMA((2,)), pltpu.SemaphoreType.DMA((2, 2)),
                      pltpu.SemaphoreType.DMA((2, 2)))

        def norm_phase(xt, xl):
            def cps(i):
                return halves(hbuf, pl.multiple_of(i * LN, LN), xt, i % 4, xl)
            for i in range(3):
                for c in cps(jnp.int32(i)):
                    c.start()
            item(FD + 4, 'yf', 'F')

            def step(i, _):
                @pl.when(i + 3 < 16)
                def _():
                    for c in cps(i + 3):
                        c.start()
                for c in cps(i):
                    c.wait()
                norm_tile(act, xt, i % 4, i * LN, 1)
                return 0
            lax.fori_loop(0, 16, step, 0)

        pl.run_scoped(norm_phase, pltpu.VMEM((4, 2, LN, HD), BF), pltpu.SemaphoreType.DMA((4, 2)))

        def ustore(n):
            return pltpu.make_async_copy(obuf.at[n % 2, :, pl.ds(0, FW)], ubuf.at[:, pl.ds(pl.multiple_of((n - F0) * FW, FW), FW)], ol.at[n % 2])

        def gate_step(n, _):
            @pl.when(n >= F0 + 2)
            def _():
                ustore(n - 2).wait()
            loaded(n, 'F')
            slot = n % SLOTS

            def mt(t, _):
                @pl.when(t == 0)
                def _():
                    item(n + YAHEAD, 'ysend', 'FG')

                    @pl.when((n == F0) | ((n - F0) * 8 // 9 > (n - F0 - 1) * 8 // 9))
                    def _():
                        item(FD + 5 + (n - F0) * 8 // 9, 'yf', 'FG')
                    item(n + 1, 'xf', 'FG')

                @pl.when(t == 1)
                def _():
                    item(n + 1, 'done', 'FGD')
                    load(n + 1, 'F')

                    @pl.when(n + 1 == G0)
                    def _():
                        for i in range(2):
                            dcopy(wdown, dl, n + 1, i).start()
                rows = pl.ds(pl.multiple_of(t * MT, MT), MT)
                acc = product(act, rows, wbuf, slot)
                gate, up = acc[:, :FW], acc[:, FW:]
                obuf[n % 2, rows, pl.ds(0, FW)] = (gate * jax.nn.sigmoid(gate) * up).astype(BF)
                return 0
            lax.fori_loop(0, TOK // MT, mt, 0)
            ustore(n).start()
            return 0
        lax.fori_loop(F0, G0, gate_step, 0)
        for n in (G0 - 2, G0 - 1):
            ustore(jnp.int32(n)).wait()

    def down_phase(wdown, dl, u, hb, yb, ul, hl, yl):
        tiles = TOK // MD

        def ucopy(t):
            rows = pl.ds(pl.multiple_of(t * MD, MD), MD)
            return pltpu.make_async_copy(ubuf.at[rows], u.at[rows], ul.at[t])

        def at(q):
            return pl.ds(pl.multiple_of((q % tiles) * MD, MD), MD), pl.ds(pl.multiple_of((q // tiles) * FW, FW), FW)

        def hcopy(q):
            return pltpu.make_async_copy(hbuf.at[at(q)], hb.at[q % 2], hl.at[q % 2])

        def ycopy(q):
            return pltpu.make_async_copy(yb.at[q % 2], y.at[at(q)], yl.at[q % 2])

        hcopy(jnp.int32(0)).start()
        for t in range(tiles):
            ucopy(t).start()

        def tile(n, t, loading):
            q = (n - G0) * tiles + t

            if loading:
                @pl.when(t % 2 == 0)
                def _():
                    item(G0 + 3 + t // 2, 'yf', 'G')
            else:
                p = q - tiles

                @pl.when((p == 0) | (4 * p // 19 > 4 * (p - 1) // 19))
                def _():
                    item(G0 + 5 + 4 * p // 19, 'yf', 'W')

            @pl.when((t == 1) & (n == N - 2))
            def _():
                item(N - 1, 'yf', 'G')

            @pl.when(t == 1)
            def _():
                item(n + 1, 'xf', 'G')

            @pl.when((t == tiles - 1) & (n + 1 < N))
            def _():
                item(n + 1, 'done', 'G')
                for i in range(2):
                    dcopy(wdown, dl, n + 1, i).start()

            @pl.when(q + 1 < NG * tiles)
            def _():
                hcopy(q + 1).start()

            @pl.when(q >= 2)
            def _():
                ycopy(q - 2).wait()
            hcopy(q).wait()
            rows = pl.ds(pl.multiple_of(t * MD, MD), MD)
            acc = None
            if loading:
                ucopy(t).wait()
            for a, b in KSPLIT:
                part = jnp.dot(u[rows, a:b], wdown[n % 2, a:b], preferred_element_type=F32)
                acc = part if acc is None else acc + part
            yb[q % 2] = (hb[q % 2].astype(F32) + acc).astype(BF)
            ycopy(q).start()

        def step(n, loading):
            for i in range(2):
                dcopy(wdown, dl, n, i).wait()

            def mt(t, _):
                tile(n, t, loading)
                return 0
            lax.fori_loop(0, tiles, mt, 0)
            return 0

        step(jnp.int32(G0), True)
        lax.fori_loop(G0 + 1, N, lambda n, _: step(n, False), 0)
        for q in (NG * tiles - 2, NG * tiles - 1):
            ycopy(jnp.int32(q)).wait()

    def last_scope(wdown, dl):
        dma = pltpu.SemaphoreType.DMA
        pl.run_scoped(functools.partial(scope, wdown, dl), pltpu.VMEM((2, TOK, HD), BF), pltpu.VMEM((SLOTS, 2, HD, CW), BF), pltpu.VMEM((2, TOK, CW), BF),
                      dma((SLOTS, 4)), dma((2,)))
        pl.run_scoped(functools.partial(down_phase, wdown, dl), pltpu.VMEM((TOK, FFN), BF), pltpu.VMEM((2, MD, FW), BF), pltpu.VMEM((2, MD, FW), BF),
                      dma((TOK // MD,)), dma((2,)), dma((2,)))

    pl.run_scoped(last_scope, pltpu.VMEM((2, FFN, FW), BF), pltpu.SemaphoreType.DMA((2, 2)))


def local_layer(x_loc, norm_attn, w_query, w_key, w_value, w_out, norm_mlp, w_gate, w_up, w_down):
    shape = x_loc.shape
    x2 = x_loc.reshape(TOK, D)
    anys = pl.BlockSpec(memory_space=pl.ANY)
    vm = pl.BlockSpec(memory_space=pltpu.VMEM)

    def out(*sh):
        return jax.ShapeDtypeStruct(sh, BF)
    sem = pltpu.SemaphoreType.DMA
    res = pl.pallas_call(
        kernel,
        out_shape=[out(TOK, D), out(ROWS * SEQ, D), out(HD, D), out(HD, D), out(HD, D), out(HD, D), out(HD, FFN), out(HD, FFN), out(HF, D),
                   out(TOK, D), out(3, ROWS * LN, HD), jax.ShapeDtypeStruct((TOK, D), F32), out(TOK, FFN), out(TOK, D)],
        in_specs=[anys, vm, vm] + [anys] * 7,
        out_specs=[anys] * 14,
        scratch_shapes=[pltpu.VMEM((2, HD // LN, LN), F32)] * 2 + [pltpu.VMEM((4, 1, HD), F32)]
        + [pltpu.VMEM((SEQ, HEAD), F32)] * 2 + [pltpu.VMEM((SEQ, LN), jnp.int32)] + [sem((YR,))] * 2 + [sem((XR,))] * 6 + [sem((2,)), sem((ROWS, 3)), sem((ROWS, 3)), sem((3,)), sem((3,))],
        compiler_params=pltpu.CompilerParams(collective_id=0, has_side_effects=True, vmem_limit_bytes=66_900_000),
        cost_estimate=pl.CostEstimate(flops=846 * 10**9, bytes_accessed=10**9, transcendentals=0),
        name='layer',
    )(x2, norm_attn.reshape(HD // LN, LN), norm_mlp.reshape(HD // LN, LN), w_query, w_key, w_value, w_out, w_gate, w_up, w_down)
    return res[0].reshape(shape)


def solution(mesh):
    rows = P(('dp', 'fsdp'), 'sp', None)
    weight = P('fsdp', None)
    gain = P('fsdp')
    specs = (rows, gain, weight, weight, weight, weight, gain, weight, weight, weight)
    return jax.shard_map(local_layer, mesh=mesh, in_specs=specs, out_specs=rows, check_vma=False)
```

time: 5660 us -> 1280 us (0.23)
  waiting for transfers between devices: 4040 us -> 0 us
  Pallas kernels: 0 us -> 1260 us
  matrix products: 1110 us -> 0 us
  other arithmetic: 325 us -> 0 us
  local copies, waits for them, and re-layouts: 161 us -> 14.1 us
    all_gather x9 -> x0, waiting for transfers between devices: 4030 us -> none  [the longest x7 3570 us: gather_weight(): return lax.all_gather(weight_shard, 'fsdp', axis=0, tiled=True)]
    pallas_call x0 -> x1, Pallas kernels: none -> 1260 us  [local_layer(): pl.pallas_call(kernel, out_shape=[out(TOK, D), out(ROWS * SEQ, D), out(HD...]
    dot_general x9 -> x0, matrix products: 1110 us -> none  [the longest x1 224 us: local_layer(): jnp.dot(hidden_mlp, gather_weight(w_down), preferred_element_type=jnp.flo...]
    another operation x1 -> x0, other arithmetic: 164 us -> none
    sub x1 -> x0, other arithmetic: 132 us -> none  [local_layer(): jax.nn.softmax(jnp.where(allowed, scores, MASK_VALUE), axis=-1)]
    slice x1 -> x0, local copies, waits for them, and re-layouts: 84.2 us -> none  [apply_rope(): lower_half = proj[..., :half_dim]]
  transfers between devices with their start and end apart: 9 -> 0, of which waited for: 9 -> 0; matrix products, arithmetic and copies ran while one was open for 24% -> 0% of each run, Pallas kernels for 0% -> 0%
where the time goes in v3:
time: 1280 us
  Pallas kernels  1260 us (98%)
  local copies, waits for them, and re-layouts  14.1 us (1%)
    pallas_call x1, Pallas kernels, local_layer(): pl.pallas_call(kernel, out_shape=[out(TOK, D), out(ROWS * SEQ, D), out(HD...  1260 us

profile of v3, /device:TPU:0, one launch (start us, length us, event | category | flops | bytes accessed | tf_op | source)
XLA Modules:
  0.0 1276.2 jit_solution(1259126542692008585)
XLA Ops:
  0.0 1262.2 %layer.1 = (bf16[2048,4096]{1,0:T(8,128)(2,1)}, bf16[4096,4096]{1,0:T(8,128)(2,1)}, bf16[2048,4096]{1,0:T(8,128)(2,1)}, bf16[2048,4096]{1,0:T(8,128)(2,1)}, bf16...) custom-call(bf16[2048,4096]{1,0:T(8,128)(2,1)} %bitcast.5, ...), custom_call_target="tpu_custom_call" | custom-call | flops 846000029696 | bytes 1000000000 | tf_op jit(solution)/shard_map/layer/pallas_call | solution.py:686
  1262.2 14.1 %copy.12 = bf16[16,128,4096]{2,1,0:T(8,128)(2,1)} copy(bf16[16,128,4096]{2,1,0:T(8,128)(2,1)} %bitcast.4) | data formatting | bytes 33554432

commit v4 on v3

--- a/solution.py
+++ b/solution.py
@@ -36,10 +36,13 @@
 FD = F0 + 3
 F_E = 512
 G_E = 1360
+G_L = 352
 YAHEAD = 16
 SLOTS = 2
 KB = 1024
-KSPLIT = ((0, 2816), (2816, 5632), (5632, 8448), (8448, FFN))
+KSPLIT = tuple(range(0, FFN - 1792, 1792)) + (FFN,)
+OWNK = 3, 1792
+RESTK = 2, 2816
 MT = 1024
 NB = 64
 MD = 512
@@ -47,7 +50,7 @@
 
 def kernel(x_in, gattn, gmlp, wq, wk, wv, wo, wg, wu, wd,
            y, xr, rq, rk, rv, ro, rg, ru, rd, ob, ostage, psum, ubuf, hbuf,
-           gown, grem, gains, cos, sin, qpos, ys, yr, xs, xrs, dys, dyr, dxs, dxr, gsem, xsend, xrecv, osend, orecv):
+           gown, grem, gains, ys, yr, xs, xrs, dys, dyr, dxs, dxr, gsem, xsend, xrecv, osend, orecv):
     f = lax.axis_index('fsdp')
     s = lax.axis_index('sp')
     cx = s // 2
@@ -150,7 +153,7 @@
         if 'W' in cand or 'G' in cand:
             when((n >= G0) & (n < N - 1), lambda: run(((wd, rd),), al((n - G0) * FW, FW), FW, HF // 2, G_E, n + 2 * NC + NF))
         if 'G' in cand:
-            when(n == N - 1, lambda: run(((wd, rd),), D - FW, FW, HF // 2, 0, n + 2 * NC + NF))
+            when(n == N - 1, lambda: run(((wd, rd),), D - FW, FW, HF // 2, G_L, n + 2 * NC + NF))
 
     gown[0] = gattn[...].astype(F32)
     gown[1] = gmlp[...].astype(F32)
@@ -174,18 +177,6 @@
         j = lax.broadcasted_iota(jnp.int32, shape, dim)
         return (j % LN) * 4 + j // LN
 
-    def table(i, _):
-        rs = pl.ds(pl.multiple_of(i * LN, LN), LN)
-        pos = lax.broadcasted_iota(jnp.int32, (LN, HEAD), 0) * 4 + i
-        lane = lax.broadcasted_iota(jnp.int32, (LN, HEAD), 1)
-        freq = jnp.exp((lane % (HEAD // 2)).astype(F32) * (-2.0 * math.log(THETA) / HEAD))
-        ang = pos.astype(F32) * freq
-        qpos[rs, :] = pos
-        cos[rs, :] = jnp.cos(ang)
-        sn = jnp.sin(ang)
-        sin[rs, :] = jnp.where(lane < HEAD // 2, -sn, sn)
-        return 0
-    lax.fori_loop(0, 4, table, 0)
     gcopy.wait_recv()
     gcopy.wait_send()
     for g in range(2):
@@ -225,7 +216,20 @@
         return rcopy(ostage.at[k - 1], ob.at[pl.ds(pl.multiple_of(first, LN), ROWS * LN), pl.ds(pl.multiple_of(cx * HD, HD), HD)],
                      osend.at[k - 1], orecv.at[k - 1], (0, f, peer(k)))
 
-    def attention_phase(act, wbuf, obuf, xt, qb, kb, vb, wl, ol, xl):
+    def attention_phase(cos, sin, qpos, act, wbuf, obuf, xt, qb, kb, vb, wl, ol, xl):
+        def table(i, _):
+            rs = pl.ds(pl.multiple_of(i * LN, LN), LN)
+            pos = lax.broadcasted_iota(jnp.int32, (LN, HEAD), 0) * 4 + i
+            lane = lax.broadcasted_iota(jnp.int32, (LN, HEAD), 1)
+            freq = jnp.exp((lane % (HEAD // 2)).astype(F32) * (-2.0 * math.log(THETA) / HEAD))
+            ang = pos.astype(F32) * freq
+            qpos[rs, :] = pos
+            cos[rs, :] = jnp.cos(ang)
+            sn = jnp.sin(ang)
+            sin[rs, :] = jnp.where(lane < HEAD // 2, -sn, sn)
+            return 0
+        lax.fori_loop(0, 4, table, 0)
+
         def wcopies(j, slot):
             cols = pl.ds(pl.multiple_of(cx * HD + j * GW, GW), GW)
             return [pltpu.make_async_copy(b.at[:, cols], wbuf.at[slot, i, :, pl.ds(t * GW, GW)], wl.at[slot, i, t])
@@ -361,7 +365,7 @@
         lax.fori_loop(0, NC, shell, 0)
         osends(jnp.int32(ROWS - 1), jnp.int32(0), jnp.int32((NC * NC - 1) % 2))
 
-    pl.run_scoped(attention_phase, pltpu.VMEM((2, ROWS * SEQ, HD), BF), pltpu.VMEM((2, 2, HD, 3 * GW), BF), pltpu.VMEM((2, SEQ, GW), BF),
+    pl.run_scoped(attention_phase, pltpu.VMEM((SEQ, HEAD), F32), pltpu.VMEM((SEQ, HEAD), F32), pltpu.VMEM((SEQ, LN), jnp.int32), pltpu.VMEM((2, ROWS * SEQ, HD), BF), pltpu.VMEM((2, 2, HD, 3 * GW), BF), pltpu.VMEM((2, SEQ, GW), BF),
                   pltpu.VMEM((4, 2, LN, HD), BF), pltpu.VMEM((SEQ, GW), BF), pltpu.VMEM((SEQ, GW), BF), pltpu.VMEM((SEQ, GW), BF),
                   pltpu.SemaphoreType.DMA((2, 2, 3)), pltpu.SemaphoreType.DMA((2, 4)), pltpu.SemaphoreType.DMA((4, 2)))
 
@@ -374,6 +378,10 @@
         cols = pl.ds(pl.multiple_of((n - G0) * FW, FW), FW)
         h = (f, 1 - f)[i]
         return pltpu.make_async_copy((wd, rd)[i].at[:, cols], wdown.at[n % 2, pl.ds(pl.multiple_of(h * HF, LN), HF)], dl.at[n % 2, i])
+
+    def ahead(wdown, dl, i):
+        slot = (G0 + 1) % 2
+        return pltpu.make_async_copy(wd.at[:, pl.ds(D - (2 - i) * FW, FW)], wdown.at[slot, pl.ds(i * HF, HF)], dl.at[slot, i])
 
     def scope(wdown, dl, act, wbuf, obuf, wl, ol):
         def wcopies(n, cand):
@@ -571,6 +579,7 @@
                     def _():
                         for i in range(2):
                             dcopy(wdown, dl, n + 1, i).start()
+                            ahead(wdown, dl, i).start()
                 rows = pl.ds(pl.multiple_of(t * MT, MT), MT)
                 acc = product(act, rows, wbuf, slot)
                 gate, up = acc[:, :FW], acc[:, FW:]
@@ -583,7 +592,7 @@
         for n in (G0 - 2, G0 - 1):
             ustore(jnp.int32(n)).wait()
 
-    def down_phase(wdown, dl, u, hb, yb, ul, hl, yl):
+    def down_phase(wdown, dl, u, hb, yb, sb, ul, hl, yl, sl):
         tiles = TOK // MD
 
         def ucopy(t):
@@ -603,64 +612,117 @@
         for t in range(tiles):
             ucopy(t).start()
 
-        def tile(n, t, loading):
+        def tail_copy(t, i):
+            rows = pl.ds(pl.multiple_of(t * MD, MD), MD)
+            return psum.at[rows, pl.ds(pl.multiple_of(D + (i - 2) * FW, FW), FW)]
+
+        def tail_store(t, i):
+            return pltpu.make_async_copy(sb.at[i], tail_copy(t, i), sl.at[i])
+
+        def tail_load(q):
+            return pltpu.make_async_copy(tail_copy(q % tiles, q // tiles - (NG - 2)), sb.at[q % 2], sl.at[q % 2])
+
+        def dots(t, slot):
+            rows = pl.ds(pl.multiple_of(t * MD, MD), MD)
+            acc = None
+            for a, b in zip(KSPLIT, KSPLIT[1:]):
+                part = jnp.dot(u[rows, a:b], wdown[slot, a:b], preferred_element_type=F32)
+                acc = part if acc is None else acc + part
+            return acc
+
+        def add_dots(i, t, ustart, wstart, slot, pieces):
+            count, k = pieces
+            rows = pl.ds(pl.multiple_of(t * MD, MD), MD)
+
+            def piece(j, _):
+                us = pl.ds(pl.multiple_of(ustart + j * k, 2 * LN), k)
+                ws = pl.ds(pl.multiple_of(wstart + j * k, LN), k)
+                sb[i] += jnp.dot(u[rows, us], wdown[slot, ws], preferred_element_type=F32)
+                return 0
+            lax.fori_loop(0, count, piece, 0)
+
+        def tile(n, t, kind):
             q = (n - G0) * tiles + t
 
-            if loading:
+            if kind == 'first':
                 @pl.when(t % 2 == 0)
                 def _():
                     item(G0 + 3 + t // 2, 'yf', 'G')
-            else:
+            elif kind == 'middle':
                 p = q - tiles
 
                 @pl.when((p == 0) | (4 * p // 19 > 4 * (p - 1) // 19))
                 def _():
                     item(G0 + 5 + 4 * p // 19, 'yf', 'W')
-
-            @pl.when((t == 1) & (n == N - 2))
-            def _():
-                item(N - 1, 'yf', 'G')
 
             @pl.when(t == 1)
             def _():
                 item(n + 1, 'xf', 'G')
 
-            @pl.when((t == tiles - 1) & (n + 1 < N))
-            def _():
+            def next_chunk():
                 item(n + 1, 'done', 'G')
                 for i in range(2):
                     dcopy(wdown, dl, n + 1, i).start()
+                if kind == 'middle':
+                    @pl.when(n == N - 3)
+                    def _():
+                        item(N - 1, 'yf', 'G')
+
+            if kind != 'first':
+                pl.when((t == tiles - 1) & (n + 1 < N))(next_chunk)
 
             @pl.when(q + 1 < NG * tiles)
             def _():
                 hcopy(q + 1).start()
+                if kind == 'last':
+                    tail_load(q + 1).start()
 
             @pl.when(q >= 2)
             def _():
                 ycopy(q - 2).wait()
             hcopy(q).wait()
-            rows = pl.ds(pl.multiple_of(t * MD, MD), MD)
-            acc = None
-            if loading:
+            if kind == 'first':
                 ucopy(t).wait()
-            for a, b in KSPLIT:
-                part = jnp.dot(u[rows, a:b], wdown[n % 2, a:b], preferred_element_type=F32)
-                acc = part if acc is None else acc + part
+            if kind == 'last':
+                tail_load(q).wait()
+                start = (1 - f) * math.prod(OWNK)
+                add_dots(q % 2, t, start, start, n % 2, RESTK)
+                acc = sb[q % 2]
+            else:
+                acc = dots(t, n % 2)
             yb[q % 2] = (hb[q % 2].astype(F32) + acc).astype(BF)
             ycopy(q).start()
-
-        def step(n, loading):
+            if kind == 'first':
+                def own(i, _):
+                    @pl.when(t > 0)
+                    def _():
+                        tail_store(t - 1, i).wait()
+                    start = math.prod(RESTK)
+                    sb[i] = jnp.zeros((MD, FW), F32)
+                    add_dots(i, t, f * start, i * HF + f * (start - HF), (G0 + 1) % 2, OWNK)
+                    tail_store(t, i).start()
+                    return 0
+                lax.fori_loop(0, 2, own, 0)
+                pl.when(t == tiles - 1)(next_chunk)
+
+        def step(n, kind):
             for i in range(2):
                 dcopy(wdown, dl, n, i).wait()
+                if kind == 'first':
+                    ahead(wdown, dl, i).wait()
 
             def mt(t, _):
-                tile(n, t, loading)
+                tile(n, t, kind)
                 return 0
             lax.fori_loop(0, tiles, mt, 0)
             return 0
 
-        step(jnp.int32(G0), True)
-        lax.fori_loop(G0 + 1, N, lambda n, _: step(n, False), 0)
+        step(jnp.int32(G0), 'first')
+        for i in range(2):
+            tail_store(tiles - 1, i).wait()
+        tail_load(jnp.int32((NG - 2) * tiles)).start()
+        lax.fori_loop(G0 + 1, N - 2, lambda n, _: step(n, 'middle'), 0)
+        lax.fori_loop(N - 2, N, lambda n, _: step(n, 'last'), 0)
         for q in (NG * tiles - 2, NG * tiles - 1):
             ycopy(jnp.int32(q)).wait()
 
@@ -669,7 +731,7 @@
         pl.run_scoped(functools.partial(scope, wdown, dl), pltpu.VMEM((2, TOK, HD), BF), pltpu.VMEM((SLOTS, 2, HD, CW), BF), pltpu.VMEM((2, TOK, CW), BF),
                       dma((SLOTS, 4)), dma((2,)))
         pl.run_scoped(functools.partial(down_phase, wdown, dl), pltpu.VMEM((TOK, FFN), BF), pltpu.VMEM((2, MD, FW), BF), pltpu.VMEM((2, MD, FW), BF),
-                      dma((TOK // MD,)), dma((2,)), dma((2,)))
+                      pltpu.VMEM((2, MD, FW), F32), dma((TOK // MD,)), dma((2,)), dma((2,)), dma((2,)))
 
     pl.run_scoped(last_scope, pltpu.VMEM((2, FFN, FW), BF), pltpu.SemaphoreType.DMA((2, 2)))
 
@@ -690,7 +752,7 @@
         in_specs=[anys, vm, vm] + [anys] * 7,
         out_specs=[anys] * 14,
         scratch_shapes=[pltpu.VMEM((2, HD // LN, LN), F32)] * 2 + [pltpu.VMEM((4, 1, HD), F32)]
-        + [pltpu.VMEM((SEQ, HEAD), F32)] * 2 + [pltpu.VMEM((SEQ, LN), jnp.int32)] + [sem((YR,))] * 2 + [sem((XR,))] * 6 + [sem((2,)), sem((ROWS, 3)), sem((ROWS, 3)), sem((3,)), sem((3,))],
+        + [sem((YR,))] * 2 + [sem((XR,))] * 6 + [sem((2,)), sem((ROWS, 3)), sem((ROWS, 3)), sem((3,)), sem((3,))],
         compiler_params=pltpu.CompilerParams(collective_id=0, has_side_effects=True, vmem_limit_bytes=66_900_000),
         cost_estimate=pl.CostEstimate(flops=846 * 10**9, bytes_accessed=10**9, transcendentals=0),
         name='layer',

time: 1280 us -> 1270 us (level)
  no operation moved by 1% of the time
where the time goes in v4:
time: 1270 us
  Pallas kernels  1250 us (98%)
  local copies, waits for them, and re-layouts  14.1 us (1%)
    pallas_call x1, Pallas kernels, local_layer(): pl.pallas_call(kernel, out_shape=[out(TOK, D), out(ROWS * SEQ, D), out(HD...  1250 us

profile of v4, /device:TPU:0, one launch (start us, length us, event | category | flops | bytes accessed | tf_op | source)
XLA Modules:
  0.0 1268.4 jit_solution(9700797602148214035)
XLA Ops:
  0.0 1254.3 %layer.1 = (bf16[2048,4096]{1,0:T(8,128)(2,1)}, bf16[4096,4096]{1,0:T(8,128)(2,1)}, bf16[2048,4096]{1,0:T(8,128)(2,1)}, bf16[2048,4096]{1,0:T(8,128)(2,1)}, bf16...) custom-call(bf16[2048,4096]{1,0:T(8,128)(2,1)} %bitcast.5, ...), custom_call_target="tpu_custom_call" | custom-call | flops 846000029696 | bytes 1000000000 | tf_op jit(solution)/shard_map/layer/pallas_call | solution.py:748
  1254.4 14.1 %copy.12 = bf16[16,128,4096]{2,1,0:T(8,128)(2,1)} copy(bf16[16,128,4096]{2,1,0:T(8,128)(2,1)} %bitcast.4) | data formatting | bytes 33554432

commit v5 on v4

--- a/solution.py
+++ b/solution.py
@@ -736,6 +736,20 @@
     pl.run_scoped(last_scope, pltpu.VMEM((2, FFN, FW), BF), pltpu.SemaphoreType.DMA((2, 2)))
 
 
+def hand_over(src, dst, buf, isem, osem):
+    count, rows, _ = buf.shape
+    parts = [pl.ds(i * rows, rows) for i in range(count)]
+    loads = [pltpu.make_async_copy(src.at[p], buf.at[i], isem.at[i]) for i, p in enumerate(parts)]
+    stores = [pltpu.make_async_copy(buf.at[i], dst.at[p], osem.at[i]) for i, p in enumerate(parts)]
+    for c in loads:
+        c.start()
+    for a, b in zip(loads, stores):
+        a.wait()
+        b.start()
+    for c in stores:
+        c.wait()
+
+
 def local_layer(x_loc, norm_attn, w_query, w_key, w_value, w_out, norm_mlp, w_gate, w_up, w_down):
     shape = x_loc.shape
     x2 = x_loc.reshape(TOK, D)
@@ -757,7 +771,17 @@
         cost_estimate=pl.CostEstimate(flops=846 * 10**9, bytes_accessed=10**9, transcendentals=0),
         name='layer',
     )(x2, norm_attn.reshape(HD // LN, LN), norm_mlp.reshape(HD // LN, LN), w_query, w_key, w_value, w_out, w_gate, w_up, w_down)
-    return res[0].reshape(shape)
+    count = 16
+    y = pl.pallas_call(
+        hand_over,
+        out_shape=out(TOK, D),
+        in_specs=[anys],
+        out_specs=anys,
+        scratch_shapes=[pltpu.VMEM((count, TOK // count, D), BF), sem((count,)), sem((count,))],
+        cost_estimate=pl.CostEstimate(flops=0, bytes_accessed=4 * TOK * D, transcendentals=0),
+        name='hand_over',
+    )(res[0])
+    return y.reshape(shape)
 
 
 def solution(mesh):

time: 1270 us -> 1270 us (level)
  Pallas kernels: 1250 us -> 1270 us
  local copies, waits for them, and re-layouts: 14.1 us -> 0 us
    unnamed x1 -> x0, local copies, waits for them, and re-layouts: 14.1 us -> none
where the time goes in v5:
time: 1270 us
  Pallas kernels  1270 us (100%)
    pallas_call x1, Pallas kernels, local_layer(): pl.pallas_call(kernel, out_shape=[out(TOK, D), out(ROWS * SEQ, D), out(HD...  1250 us

profile of v5, /device:TPU:0, one launch (start us, length us, event | category | flops | bytes accessed | tf_op | source)
XLA Modules:
  0.0 1266.5 jit_solution(10306011441591682198)
XLA Ops:
  0.0 1254.3 %layer.1 = (bf16[2048,4096]{1,0:T(8,128)(2,1)}, bf16[4096,4096]{1,0:T(8,128)(2,1)}, bf16[2048,4096]{1,0:T(8,128)(2,1)}, bf16[2048,4096]{1,0:T(8,128)(2,1)}, bf16...) custom-call(bf16[2048,4096]{1,0:T(8,128)(2,1)} %bitcast.4, ...), custom_call_target="tpu_custom_call" | custom-call | flops 846000029696 | bytes 1000000000 | tf_op jit(solution)/shard_map/layer/pallas_call | solution.py:762
  1254.4 12.0 hand_over.1
